TPU v7x, 32 devices: a whole 2x2x4 slice. The times are simulated.
32 devices in a mesh: gx: 4 (over y, core), gy: 4 (over z), gz: 2 (over x).
Axes of the slice: x: 2, y: 2, z: 4, core: 2. Of those that a mesh axis runs over, the one named last changes fastest.
Arguments:
- positions: float32 [3, 8, 8, 4, 256], P(None, 'gx', 'gy', 'gz'), may hold values from 0 to 1
- velocities: float32 [3, 8, 8, 4, 256], P(None, 'gx', 'gy', 'gz'), may hold values from -3 to 3
- masses: float32 [8, 8, 4, 256], P('gx', 'gy', 'gz'), may hold values from 0.0025 to 0.01
- entropy: float32 [8, 8, 4, 256], P('gx', 'gy', 'gz'), may hold values from 0.5 to 2
- counts: int32 [8, 8, 4], P('gx', 'gy', 'gz'), may hold values from 8 to 256, as said below
Outputs:
- density: float32 [8, 8, 4, 256], P('gx', 'gy', 'gz')
- acceleration: float32 [3, 8, 8, 4, 256], P(None, 'gx', 'gy', 'gz')
Inputs may be any that keep to these rules, and one draw needn't show every extreme that they name: The first counts[c] slots of cell c hold particles; the other slots of the cell are padding whose values are arbitrary.
All inputs are finite; a program needn't handle non-finite values.
Results may differ from a plain program's by a relative error of at most 0.0003.
Values sent between devices are 32-bit elements; how exact they have to be, the bound alone decides.
No kernel may reach another device: no remote copies, remote signals or barrier semaphores. Data moves between devices by JAX's collectives and lax.ppermute only.
A program may use at most 64 MiB of HBM per device.

v0:
```python
import math

import jax
import jax.numpy as jnp
from jax import lax
from jax.sharding import PartitionSpec as P

SIGMA = 8.0 / math.pi
GAMMA = 5.0 / 3.0
ALPHA = 1.0
BETA = 2.0
SOFTEN = 0.01


def with_halo(block, sides, width):
    for axis, dim in sides:
        count = lax.axis_size(axis)
        forward = [(i, i + 1) for i in range(count - 1)]
        forward.append((count - 1, 0))
        backward = [(target, source) for source, target in forward]
        low = lax.ppermute(
            lax.slice_in_dim(block, block.shape[dim] - width, None, axis=dim), axis, forward
        )
        high = lax.ppermute(lax.slice_in_dim(block, 0, width, axis=dim), axis, backward)
        block = jnp.concatenate([low, block, high], axis=dim)
    return block


def kernel_value(radius_sq):
    radius = jnp.sqrt(radius_sq)
    near_part = 1.0 - 6.0 * radius * radius + 6.0 * radius * radius * radius
    far_part = 2.0 * (1.0 - radius) ** 3
    return SIGMA * jnp.where(radius < 0.5, near_part, jnp.where(radius < 1.0, far_part, 0.0))


def kernel_slope(radius_sq):
    radius = jnp.sqrt(radius_sq)
    near_part = -12.0 + 18.0 * radius
    far_part = -6.0 * (1.0 - radius) ** 2 / jnp.maximum(radius, 0.5)
    return SIGMA * jnp.where(radius < 0.5, near_part, jnp.where(radius < 1.0, far_part, 0.0))


def block_of(values, start_x, start_y, start_z, size_x, size_y, size_z):
    leading = values.shape[:-4]
    anchor = jnp.zeros((), jnp.int32)
    starts = (anchor,) * len(leading) + (start_x, start_y, start_z, anchor)
    return lax.dynamic_slice(values, starts, leading + (size_x, size_y, size_z, values.shape[-1]))


def flatten(values):
    return values.reshape(values.shape[:-4] + (-1, values.shape[-1]))


def offsets(number):
    number = jnp.asarray(number).astype(jnp.int32)
    return (number // 9, number // 3 % 3, number % 3)


def density_sum(targets, grid_pos, grid_weight):
    size_x, size_y, size_z = (grid_pos.shape[1] - 2, grid_pos.shape[2] - 2, grid_pos.shape[3] - 2)
    picked = jnp.moveaxis(targets, 1, 0)

    def density_add_cells(number, running):
        step_x, step_y, step_z = offsets(number)
        source = jnp.moveaxis(
            flatten(block_of(grid_pos, step_x, step_y, step_z, size_x, size_y, size_z)), 1, 0
        )
        source_weight = flatten(
            block_of(grid_weight, step_x, step_y, step_z, size_x, size_y, size_z)
        )
        displace = jnp.stack([step_x, step_y, step_z]).astype(jnp.float32) - 1.0

        def density_one_cell(items):
            own, far, far_weight = items
            between = own[:, :, None] - far[:, None, :] - displace[:, None, None]
            radius_sq = jnp.sum(between * between, 0)
            return jnp.sum(far_weight[None, :] * kernel_value(radius_sq), 1)

        return running + lax.map(density_one_cell, (picked, source, source_weight))

    return lax.fori_loop(
        0, 27, density_add_cells, jnp.zeros((picked.shape[0], picked.shape[2]), jnp.float32)
    )


def force_sum(targets, margins):
    own_pos, own_vel, own_rho, own_sound, own_press = [item for item in targets]
    own_pos = jnp.moveaxis(own_pos, 1, 0)
    own_vel = jnp.moveaxis(own_vel, 1, 0)
    size_x, size_y, size_z = (
        margins[0].shape[1] - 2,
        margins[0].shape[2] - 2,
        margins[0].shape[3] - 2,
    )

    def force_add_cells(number, running):
        step_x, step_y, step_z = offsets(number)
        pieces = [
            flatten(block_of(item, step_x, step_y, step_z, size_x, size_y, size_z))
            for item in margins
        ]
        far_pos, far_vel, far_weight, far_rho, far_sound, far_press = pieces
        far_pos = jnp.moveaxis(far_pos, 1, 0)
        far_vel = jnp.moveaxis(far_vel, 1, 0)
        displace = jnp.stack([step_x, step_y, step_z]).astype(jnp.float32) - 1.0

        def force_one_cell(items):
            (
                mine_pos,
                mine_vel,
                mine_rho,
                mine_sound,
                mine_press,
                other_pos,
                other_vel,
                other_weight,
                other_rho,
                other_sound,
                other_press,
            ) = items
            between = mine_pos[:, :, None] - other_pos[:, None, :] - displace[:, None, None]
            radius_sq = jnp.sum(between * between, 0)
            closing = jnp.sum((mine_vel[:, :, None] - other_vel[:, None, :]) * between, 0)
            approach = jnp.minimum(closing, 0.0) / (radius_sq + SOFTEN)
            mean_sound = 0.5 * (mine_sound[:, None] + other_sound[None, :])
            mean_rho = 0.5 * (mine_rho[:, None] + other_rho[None, :])
            viscous = (BETA * approach * approach - ALPHA * mean_sound * approach) / mean_rho
            factor = (
                other_weight[None, :]
                * (mine_press[:, None] + other_press[None, :] + viscous)
                * kernel_slope(radius_sq)
            )
            return jnp.sum(factor[None] * between, 2)

        items = (
            own_pos,
            own_vel,
            own_rho,
            own_sound,
            own_press,
            far_pos,
            far_vel,
            far_weight,
            far_rho,
            far_sound,
            far_press,
        )
        return running - lax.map(force_one_cell, items)

    total = lax.fori_loop(0, 27, force_add_cells, jnp.zeros(own_pos.shape, jnp.float32))
    return jnp.moveaxis(total, 0, 1)


def states_of(safe_density, entropy):
    pressure_term = entropy * safe_density ** (GAMMA - 2.0)
    sound_speed = jnp.sqrt(GAMMA * entropy * safe_density ** (GAMMA - 1.0))
    return (pressure_term, sound_speed)


def per_device(positions, velocities, masses, entropy, counts):
    size_x, size_y, size_z, slots = masses.shape
    cell_total = size_x * size_y * size_z
    slot_ids = lax.broadcasted_iota(jnp.int32, masses.shape, 3)
    active = slot_ids < counts[..., None]
    weight = jnp.where(active, masses, 0.0)
    flat_active = active.reshape(cell_total, slots)
    flat_entropy = entropy.reshape(cell_total, slots)
    own_pos = positions.reshape(3, cell_total, slots)
    own_vel = velocities.reshape(3, cell_total, slots)
    packed = jnp.concatenate([positions, velocities, weight[None]], 0)
    nearby = with_halo(packed, (("gx", 1), ("gy", 2), ("gz", 3)), 1)
    raw_density = density_sum(own_pos, nearby[0:3], nearby[6])
    own_safe = jnp.where(flat_active, raw_density, 1.0)
    own_press, own_sound = states_of(own_safe, flat_entropy)
    scalars = jnp.stack([own_safe, own_sound, own_press]).reshape(
        (3, size_x, size_y, size_z, slots)
    )
    fields = with_halo(scalars, (("gx", 1), ("gy", 2), ("gz", 3)), 1)
    margins = (nearby[0:3], nearby[3:6], nearby[6], fields[0], fields[1], fields[2])
    targets = (own_pos, own_vel, own_safe, own_sound, own_press)
    raw_accel = force_sum(targets, margins)
    density = jnp.where(flat_active, raw_density, 0.0).reshape(masses.shape)
    acceleration = jnp.where(flat_active[None], raw_accel, 0.0).reshape(positions.shape)
    return (density, acceleration)


def solution(mesh):
    return jax.shard_map(
        per_device,
        mesh=mesh,
        in_specs=(
            P(None, "gx", "gy", "gz", None),
            P(None, "gx", "gy", "gz", None),
            P("gx", "gy", "gz", None),
            P("gx", "gy", "gz", None),
            P("gx", "gy", "gz"),
        ),
        out_specs=(P("gx", "gy", "gz", None), P(None, "gx", "gy", "gz", None)),
        check_vma=False,
    )
```

profile of v0, /device:TPU:0, one launch (start us, length us, event | category | flops | bytes accessed | tf_op | source)
XLA Modules:
  0.0 410.2 jit_solution(3773107644210119053)
XLA Ops:
  2.8 2.0 collective-permute-start.1
  6.5 2.3 collective-permute-start.2
  8.8 2.1 collective-permute-start.3
  10.9 2.2 collective-permute-done.2
  17.9 3.2 collective-permute-done.4
  23.2 123.9 %while.111 = (s32[]{:T(128)}, f32[8,256]{1,0:T(8,128)S(1)}, f32[3,4,4,4,256]{4,0,3,2,1:T(4,128)S(1)}, f32[4,4,4,256]{3,2,1,0:T(4,128)S(1)}, f32[8,3,256]{2,1,0:T...) while((s32[]{:T(128)}, f32[8,256]{1,0:T(8,128)S(1)}, ...), condition=%wide.region_5.6_spmd.clone.clone, body=%wide.region_0.5_spmd.clone.sunk.clone | while | flops 1708082 | bytes 656052 | solution.py:81
  23.5 4.3 %while.110 = (s32[]{:T(128)}, f32[8,256]{1,0:T(8,128)S(1)}, f32[8,3,256]{2,1,0:T(4,128)S(1)}, f32[8,3,256]{2,1,0:T(4,128)S(1)}, f32[3]{0:T(128)S(1)}, /*index=5*/f32[8,256]{1,0:T(8,128)S(1)}, s32[]{:T(128)}, s32[]{:T(128)}) while((s32[]{:T(128)}, f32[8,256]{1,0:T(8,128)S(1)}, f32[8,3,256]{2,1,0:T(4,128)S(1)}, f32[8,3,256]{2,1,0:T(4,128)S(1)}, ...), condition=%wide.region_4.4_spmd, body=%wide.region_1.3_spmd.sunk | while | flops 1703938 | bytes 548973 | solution.py:79
  28.1 4.3 %while.110 = (s32[]{:T(128)}, f32[8,256]{1,0:T(8,128)S(1)}, f32[8,3,256]{2,1,0:T(4,128)S(1)}, f32[8,3,256]{2,1,0:T(4,128)S(1)}, f32[3]{0:T(128)S(1)}, /*index=5*/f32[8,256]{1,0:T(8,128)S(1)}, s32[]{:T(128)}, s32[]{:T(128)}) while((s32[]{:T(128)}, f32[8,256]{1,0:T(8,128)S(1)}, f32[8,3,256]{2,1,0:T(4,128)S(1)}, f32[8,3,256]{2,1,0:T(4,128)S(1)}, ...), condition=%wide.region_4.4_spmd, body=%wide.region_1.3_spmd.sunk | while | flops 1703938 | bytes 548973 | solution.py:79
  32.7 4.3 %while.110 = (s32[]{:T(128)}, f32[8,256]{1,0:T(8,128)S(1)}, f32[8,3,256]{2,1,0:T(4,128)S(1)}, f32[8,3,256]{2,1,0:T(4,128)S(1)}, f32[3]{0:T(128)S(1)}, /*index=5*/f32[8,256]{1,0:T(8,128)S(1)}, s32[]{:T(128)}, s32[]{:T(128)}) while((s32[]{:T(128)}, f32[8,256]{1,0:T(8,128)S(1)}, f32[8,3,256]{2,1,0:T(4,128)S(1)}, f32[8,3,256]{2,1,0:T(4,128)S(1)}, ...), condition=%wide.region_4.4_spmd, body=%wide.region_1.3_spmd.sunk | while | flops 1703938 | bytes 548973 | solution.py:79
  37.2 4.3 %while.110 = (s32[]{:T(128)}, f32[8,256]{1,0:T(8,128)S(1)}, f32[8,3,256]{2,1,0:T(4,128)S(1)}, f32[8,3,256]{2,1,0:T(4,128)S(1)}, f32[3]{0:T(128)S(1)}, /*index=5*/f32[8,256]{1,0:T(8,128)S(1)}, s32[]{:T(128)}, s32[]{:T(128)}) while((s32[]{:T(128)}, f32[8,256]{1,0:T(8,128)S(1)}, f32[8,3,256]{2,1,0:T(4,128)S(1)}, f32[8,3,256]{2,1,0:T(4,128)S(1)}, ...), condition=%wide.region_4.4_spmd, body=%wide.region_1.3_spmd.sunk | while | flops 1703938 | bytes 548973 | solution.py:79
  41.8 4.3 %while.110 = (s32[]{:T(128)}, f32[8,256]{1,0:T(8,128)S(1)}, f32[8,3,256]{2,1,0:T(4,128)S(1)}, f32[8,3,256]{2,1,0:T(4,128)S(1)}, f32[3]{0:T(128)S(1)}, /*index=5*/f32[8,256]{1,0:T(8,128)S(1)}, s32[]{:T(128)}, s32[]{:T(128)}) while((s32[]{:T(128)}, f32[8,256]{1,0:T(8,128)S(1)}, f32[8,3,256]{2,1,0:T(4,128)S(1)}, f32[8,3,256]{2,1,0:T(4,128)S(1)}, ...), condition=%wide.region_4.4_spmd, body=%wide.region_1.3_spmd.sunk | while | flops 1703938 | bytes 548973 | solution.py:79
  46.4 4.3 %while.110 = (s32[]{:T(128)}, f32[8,256]{1,0:T(8,128)S(1)}, f32[8,3,256]{2,1,0:T(4,128)S(1)}, f32[8,3,256]{2,1,0:T(4,128)S(1)}, f32[3]{0:T(128)S(1)}, /*index=5*/f32[8,256]{1,0:T(8,128)S(1)}, s32[]{:T(128)}, s32[]{:T(128)}) while((s32[]{:T(128)}, f32[8,256]{1,0:T(8,128)S(1)}, f32[8,3,256]{2,1,0:T(4,128)S(1)}, f32[8,3,256]{2,1,0:T(4,128)S(1)}, ...), condition=%wide.region_4.4_spmd, body=%wide.region_1.3_spmd.sunk | while | flops 1703938 | bytes 548973 | solution.py:79
  51.0 4.3 %while.110 = (s32[]{:T(128)}, f32[8,256]{1,0:T(8,128)S(1)}, f32[8,3,256]{2,1,0:T(4,128)S(1)}, f32[8,3,256]{2,1,0:T(4,128)S(1)}, f32[3]{0:T(128)S(1)}, /*index=5*/f32[8,256]{1,0:T(8,128)S(1)}, s32[]{:T(128)}, s32[]{:T(128)}) while((s32[]{:T(128)}, f32[8,256]{1,0:T(8,128)S(1)}, f32[8,3,256]{2,1,0:T(4,128)S(1)}, f32[8,3,256]{2,1,0:T(4,128)S(1)}, ...), condition=%wide.region_4.4_spmd, body=%wide.region_1.3_spmd.sunk | while | flops 1703938 | bytes 548973 | solution.py:79
  55.6 4.3 %while.110 = (s32[]{:T(128)}, f32[8,256]{1,0:T(8,128)S(1)}, f32[8,3,256]{2,1,0:T(4,128)S(1)}, f32[8,3,256]{2,1,0:T(4,128)S(1)}, f32[3]{0:T(128)S(1)}, /*index=5*/f32[8,256]{1,0:T(8,128)S(1)}, s32[]{:T(128)}, s32[]{:T(128)}) while((s32[]{:T(128)}, f32[8,256]{1,0:T(8,128)S(1)}, f32[8,3,256]{2,1,0:T(4,128)S(1)}, f32[8,3,256]{2,1,0:T(4,128)S(1)}, ...), condition=%wide.region_4.4_spmd, body=%wide.region_1.3_spmd.sunk | while | flops 1703938 | bytes 548973 | solution.py:79
  60.2 4.3 %while.110 = (s32[]{:T(128)}, f32[8,256]{1,0:T(8,128)S(1)}, f32[8,3,256]{2,1,0:T(4,128)S(1)}, f32[8,3,256]{2,1,0:T(4,128)S(1)}, f32[3]{0:T(128)S(1)}, /*index=5*/f32[8,256]{1,0:T(8,128)S(1)}, s32[]{:T(128)}, s32[]{:T(128)}) while((s32[]{:T(128)}, f32[8,256]{1,0:T(8,128)S(1)}, f32[8,3,256]{2,1,0:T(4,128)S(1)}, f32[8,3,256]{2,1,0:T(4,128)S(1)}, ...), condition=%wide.region_4.4_spmd, body=%wide.region_1.3_spmd.sunk | while | flops 1703938 | bytes 548973 | solution.py:79
  64.8 4.3 %while.110 = (s32[]{:T(128)}, f32[8,256]{1,0:T(8,128)S(1)}, f32[8,3,256]{2,1,0:T(4,128)S(1)}, f32[8,3,256]{2,1,0:T(4,128)S(1)}, f32[3]{0:T(128)S(1)}, /*index=5*/f32[8,256]{1,0:T(8,128)S(1)}, s32[]{:T(128)}, s32[]{:T(128)}) while((s32[]{:T(128)}, f32[8,256]{1,0:T(8,128)S(1)}, f32[8,3,256]{2,1,0:T(4,128)S(1)}, f32[8,3,256]{2,1,0:T(4,128)S(1)}, ...), condition=%wide.region_4.4_spmd, body=%wide.region_1.3_spmd.sunk | while | flops 1703938 | bytes 548973 | solution.py:79
  69.4 4.3 %while.110 = (s32[]{:T(128)}, f32[8,256]{1,0:T(8,128)S(1)}, f32[8,3,256]{2,1,0:T(4,128)S(1)}, f32[8,3,256]{2,1,0:T(4,128)S(1)}, f32[3]{0:T(128)S(1)}, /*index=5*/f32[8,256]{1,0:T(8,128)S(1)}, s32[]{:T(128)}, s32[]{:T(128)}) while((s32[]{:T(128)}, f32[8,256]{1,0:T(8,128)S(1)}, f32[8,3,256]{2,1,0:T(4,128)S(1)}, f32[8,3,256]{2,1,0:T(4,128)S(1)}, ...), condition=%wide.region_4.4_spmd, body=%wide.region_1.3_spmd.sunk | while | flops 1703938 | bytes 548973 | solution.py:79
  73.9 4.3 %while.110 = (s32[]{:T(128)}, f32[8,256]{1,0:T(8,128)S(1)}, f32[8,3,256]{2,1,0:T(4,128)S(1)}, f32[8,3,256]{2,1,0:T(4,128)S(1)}, f32[3]{0:T(128)S(1)}, /*index=5*/f32[8,256]{1,0:T(8,128)S(1)}, s32[]{:T(128)}, s32[]{:T(128)}) while((s32[]{:T(128)}, f32[8,256]{1,0:T(8,128)S(1)}, f32[8,3,256]{2,1,0:T(4,128)S(1)}, f32[8,3,256]{2,1,0:T(4,128)S(1)}, ...), condition=%wide.region_4.4_spmd, body=%wide.region_1.3_spmd.sunk | while | flops 1703938 | bytes 548973 | solution.py:79
  78.5 4.3 %while.110 = (s32[]{:T(128)}, f32[8,256]{1,0:T(8,128)S(1)}, f32[8,3,256]{2,1,0:T(4,128)S(1)}, f32[8,3,256]{2,1,0:T(4,128)S(1)}, f32[3]{0:T(128)S(1)}, /*index=5*/f32[8,256]{1,0:T(8,128)S(1)}, s32[]{:T(128)}, s32[]{:T(128)}) while((s32[]{:T(128)}, f32[8,256]{1,0:T(8,128)S(1)}, f32[8,3,256]{2,1,0:T(4,128)S(1)}, f32[8,3,256]{2,1,0:T(4,128)S(1)}, ...), condition=%wide.region_4.4_spmd, body=%wide.region_1.3_spmd.sunk | while | flops 1703938 | bytes 548973 | solution.py:79
  83.1 4.3 %while.110 = (s32[]{:T(128)}, f32[8,256]{1,0:T(8,128)S(1)}, f32[8,3,256]{2,1,0:T(4,128)S(1)}, f32[8,3,256]{2,1,0:T(4,128)S(1)}, f32[3]{0:T(128)S(1)}, /*index=5*/f32[8,256]{1,0:T(8,128)S(1)}, s32[]{:T(128)}, s32[]{:T(128)}) while((s32[]{:T(128)}, f32[8,256]{1,0:T(8,128)S(1)}, f32[8,3,256]{2,1,0:T(4,128)S(1)}, f32[8,3,256]{2,1,0:T(4,128)S(1)}, ...), condition=%wide.region_4.4_spmd, body=%wide.region_1.3_spmd.sunk | while | flops 1703938 | bytes 548973 | solution.py:79
  87.7 4.3 %while.110 = (s32[]{:T(128)}, f32[8,256]{1,0:T(8,128)S(1)}, f32[8,3,256]{2,1,0:T(4,128)S(1)}, f32[8,3,256]{2,1,0:T(4,128)S(1)}, f32[3]{0:T(128)S(1)}, /*index=5*/f32[8,256]{1,0:T(8,128)S(1)}, s32[]{:T(128)}, s32[]{:T(128)}) while((s32[]{:T(128)}, f32[8,256]{1,0:T(8,128)S(1)}, f32[8,3,256]{2,1,0:T(4,128)S(1)}, f32[8,3,256]{2,1,0:T(4,128)S(1)}, ...), condition=%wide.region_4.4_spmd, body=%wide.region_1.3_spmd.sunk | while | flops 1703938 | bytes 548973 | solution.py:79
  92.3 4.3 %while.110 = (s32[]{:T(128)}, f32[8,256]{1,0:T(8,128)S(1)}, f32[8,3,256]{2,1,0:T(4,128)S(1)}, f32[8,3,256]{2,1,0:T(4,128)S(1)}, f32[3]{0:T(128)S(1)}, /*index=5*/f32[8,256]{1,0:T(8,128)S(1)}, s32[]{:T(128)}, s32[]{:T(128)}) while((s32[]{:T(128)}, f32[8,256]{1,0:T(8,128)S(1)}, f32[8,3,256]{2,1,0:T(4,128)S(1)}, f32[8,3,256]{2,1,0:T(4,128)S(1)}, ...), condition=%wide.region_4.4_spmd, body=%wide.region_1.3_spmd.sunk | while | flops 1703938 | bytes 548973 | solution.py:79
  96.9 4.3 %while.110 = (s32[]{:T(128)}, f32[8,256]{1,0:T(8,128)S(1)}, f32[8,3,256]{2,1,0:T(4,128)S(1)}, f32[8,3,256]{2,1,0:T(4,128)S(1)}, f32[3]{0:T(128)S(1)}, /*index=5*/f32[8,256]{1,0:T(8,128)S(1)}, s32[]{:T(128)}, s32[]{:T(128)}) while((s32[]{:T(128)}, f32[8,256]{1,0:T(8,128)S(1)}, f32[8,3,256]{2,1,0:T(4,128)S(1)}, f32[8,3,256]{2,1,0:T(4,128)S(1)}, ...), condition=%wide.region_4.4_spmd, body=%wide.region_1.3_spmd.sunk | while | flops 1703938 | bytes 548973 | solution.py:79
  101.5 4.3 %while.110 = (s32[]{:T(128)}, f32[8,256]{1,0:T(8,128)S(1)}, f32[8,3,256]{2,1,0:T(4,128)S(1)}, f32[8,3,256]{2,1,0:T(4,128)S(1)}, f32[3]{0:T(128)S(1)}, /*index=5*/f32[8,256]{1,0:T(8,128)S(1)}, s32[]{:T(128)}, s32[]{:T(128)}) while((s32[]{:T(128)}, f32[8,256]{1,0:T(8,128)S(1)}, f32[8,3,256]{2,1,0:T(4,128)S(1)}, f32[8,3,256]{2,1,0:T(4,128)S(1)}, ...), condition=%wide.region_4.4_spmd, body=%wide.region_1.3_spmd.sunk | while | flops 1703938 | bytes 548973 | solution.py:79
  106.1 4.3 %while.110 = (s32[]{:T(128)}, f32[8,256]{1,0:T(8,128)S(1)}, f32[8,3,256]{2,1,0:T(4,128)S(1)}, f32[8,3,256]{2,1,0:T(4,128)S(1)}, f32[3]{0:T(128)S(1)}, /*index=5*/f32[8,256]{1,0:T(8,128)S(1)}, s32[]{:T(128)}, s32[]{:T(128)}) while((s32[]{:T(128)}, f32[8,256]{1,0:T(8,128)S(1)}, f32[8,3,256]{2,1,0:T(4,128)S(1)}, f32[8,3,256]{2,1,0:T(4,128)S(1)}, ...), condition=%wide.region_4.4_spmd, body=%wide.region_1.3_spmd.sunk | while | flops 1703938 | bytes 548973 | solution.py:79
  110.7 4.3 %while.110 = (s32[]{:T(128)}, f32[8,256]{1,0:T(8,128)S(1)}, f32[8,3,256]{2,1,0:T(4,128)S(1)}, f32[8,3,256]{2,1,0:T(4,128)S(1)}, f32[3]{0:T(128)S(1)}, /*index=5*/f32[8,256]{1,0:T(8,128)S(1)}, s32[]{:T(128)}, s32[]{:T(128)}) while((s32[]{:T(128)}, f32[8,256]{1,0:T(8,128)S(1)}, f32[8,3,256]{2,1,0:T(4,128)S(1)}, f32[8,3,256]{2,1,0:T(4,128)S(1)}, ...), condition=%wide.region_4.4_spmd, body=%wide.region_1.3_spmd.sunk | while | flops 1703938 | bytes 548973 | solution.py:79
  115.2 4.3 %while.110 = (s32[]{:T(128)}, f32[8,256]{1,0:T(8,128)S(1)}, f32[8,3,256]{2,1,0:T(4,128)S(1)}, f32[8,3,256]{2,1,0:T(4,128)S(1)}, f32[3]{0:T(128)S(1)}, /*index=5*/f32[8,256]{1,0:T(8,128)S(1)}, s32[]{:T(128)}, s32[]{:T(128)}) while((s32[]{:T(128)}, f32[8,256]{1,0:T(8,128)S(1)}, f32[8,3,256]{2,1,0:T(4,128)S(1)}, f32[8,3,256]{2,1,0:T(4,128)S(1)}, ...), condition=%wide.region_4.4_spmd, body=%wide.region_1.3_spmd.sunk | while | flops 1703938 | bytes 548973 | solution.py:79
  119.8 4.3 %while.110 = (s32[]{:T(128)}, f32[8,256]{1,0:T(8,128)S(1)}, f32[8,3,256]{2,1,0:T(4,128)S(1)}, f32[8,3,256]{2,1,0:T(4,128)S(1)}, f32[3]{0:T(128)S(1)}, /*index=5*/f32[8,256]{1,0:T(8,128)S(1)}, s32[]{:T(128)}, s32[]{:T(128)}) while((s32[]{:T(128)}, f32[8,256]{1,0:T(8,128)S(1)}, f32[8,3,256]{2,1,0:T(4,128)S(1)}, f32[8,3,256]{2,1,0:T(4,128)S(1)}, ...), condition=%wide.region_4.4_spmd, body=%wide.region_1.3_spmd.sunk | while | flops 1703938 | bytes 548973 | solution.py:79
  124.4 4.3 %while.110 = (s32[]{:T(128)}, f32[8,256]{1,0:T(8,128)S(1)}, f32[8,3,256]{2,1,0:T(4,128)S(1)}, f32[8,3,256]{2,1,0:T(4,128)S(1)}, f32[3]{0:T(128)S(1)}, /*index=5*/f32[8,256]{1,0:T(8,128)S(1)}, s32[]{:T(128)}, s32[]{:T(128)}) while((s32[]{:T(128)}, f32[8,256]{1,0:T(8,128)S(1)}, f32[8,3,256]{2,1,0:T(4,128)S(1)}, f32[8,3,256]{2,1,0:T(4,128)S(1)}, ...), condition=%wide.region_4.4_spmd, body=%wide.region_1.3_spmd.sunk | while | flops 1703938 | bytes 548973 | solution.py:79
  129.0 4.3 %while.110 = (s32[]{:T(128)}, f32[8,256]{1,0:T(8,128)S(1)}, f32[8,3,256]{2,1,0:T(4,128)S(1)}, f32[8,3,256]{2,1,0:T(4,128)S(1)}, f32[3]{0:T(128)S(1)}, /*index=5*/f32[8,256]{1,0:T(8,128)S(1)}, s32[]{:T(128)}, s32[]{:T(128)}) while((s32[]{:T(128)}, f32[8,256]{1,0:T(8,128)S(1)}, f32[8,3,256]{2,1,0:T(4,128)S(1)}, f32[8,3,256]{2,1,0:T(4,128)S(1)}, ...), condition=%wide.region_4.4_spmd, body=%wide.region_1.3_spmd.sunk | while | flops 1703938 | bytes 548973 | solution.py:79
  133.6 4.3 %while.110 = (s32[]{:T(128)}, f32[8,256]{1,0:T(8,128)S(1)}, f32[8,3,256]{2,1,0:T(4,128)S(1)}, f32[8,3,256]{2,1,0:T(4,128)S(1)}, f32[3]{0:T(128)S(1)}, /*index=5*/f32[8,256]{1,0:T(8,128)S(1)}, s32[]{:T(128)}, s32[]{:T(128)}) while((s32[]{:T(128)}, f32[8,256]{1,0:T(8,128)S(1)}, f32[8,3,256]{2,1,0:T(4,128)S(1)}, f32[8,3,256]{2,1,0:T(4,128)S(1)}, ...), condition=%wide.region_4.4_spmd, body=%wide.region_1.3_spmd.sunk | while | flops 1703938 | bytes 548973 | solution.py:79
  138.2 4.3 %while.110 = (s32[]{:T(128)}, f32[8,256]{1,0:T(8,128)S(1)}, f32[8,3,256]{2,1,0:T(4,128)S(1)}, f32[8,3,256]{2,1,0:T(4,128)S(1)}, f32[3]{0:T(128)S(1)}, /*index=5*/f32[8,256]{1,0:T(8,128)S(1)}, s32[]{:T(128)}, s32[]{:T(128)}) while((s32[]{:T(128)}, f32[8,256]{1,0:T(8,128)S(1)}, f32[8,3,256]{2,1,0:T(4,128)S(1)}, f32[8,3,256]{2,1,0:T(4,128)S(1)}, ...), condition=%wide.region_4.4_spmd, body=%wide.region_1.3_spmd.sunk | while | flops 1703938 | bytes 548973 | solution.py:79
  142.8 4.3 %while.110 = (s32[]{:T(128)}, f32[8,256]{1,0:T(8,128)S(1)}, f32[8,3,256]{2,1,0:T(4,128)S(1)}, f32[8,3,256]{2,1,0:T(4,128)S(1)}, f32[3]{0:T(128)S(1)}, /*index=5*/f32[8,256]{1,0:T(8,128)S(1)}, s32[]{:T(128)}, s32[]{:T(128)}) while((s32[]{:T(128)}, f32[8,256]{1,0:T(8,128)S(1)}, f32[8,3,256]{2,1,0:T(4,128)S(1)}, f32[8,3,256]{2,1,0:T(4,128)S(1)}, ...), condition=%wide.region_4.4_spmd, body=%wide.region_1.3_spmd.sunk | while | flops 1703938 | bytes 548973 | solution.py:79
  151.6 2.9 collective-permute-start.9
  154.5 1.8 collective-permute-done.8
  159.2 1.8 collective-permute-done.10
  162.1 247.4 %while.113 = (s32[]{:T(128)}, f32[8,3,256]{2,1,0:T(4,128)S(1)}, f32[3,4,4,4,256]{4,0,3,2,1:T(4,128)S(1)}, f32[3,4,4,4,256]{4,3,2,1,0:T(4,128)S(1)}, f32[4,4,4,25...) while((s32[]{:T(128)}, f32[8,3,256]{2,1,0:T(4,128)S(1)}, ...), condition=%wide.region_12.13_spmd.clone.clone, body=%wide.region_6.12_spmd.clone.sunk.clone | while | flops 3878194 | bytes 2001816 | solution.py:150
  162.5 8.7 %while.112 = (s32[]{:T(128)}, f32[8,3,256]{2,1,0:T(4,128)S(1)}, f32[8,256]{1,0:T(8,128)S(1)}, f32[8,256]{1,0:T(8,128)S(1)}, f32[8,256]{1,0:T(8,128)S(1)}, /*inde...) while((s32[]{:T(128)}, f32[8,3,256]{2,1,0:T(4,128)S(1)}, ...), condition=%wide.region_11.11_spmd, body=%wide.region_7.10_spmd.sunk | while | flops 3865858 | bytes 1648833 | solution.py:148
  171.6 8.7 %while.112 = (s32[]{:T(128)}, f32[8,3,256]{2,1,0:T(4,128)S(1)}, f32[8,256]{1,0:T(8,128)S(1)}, f32[8,256]{1,0:T(8,128)S(1)}, f32[8,256]{1,0:T(8,128)S(1)}, /*inde...) while((s32[]{:T(128)}, f32[8,3,256]{2,1,0:T(4,128)S(1)}, ...), condition=%wide.region_11.11_spmd, body=%wide.region_7.10_spmd.sunk | while | flops 3865858 | bytes 1648833 | solution.py:148
  180.8 8.7 %while.112 = (s32[]{:T(128)}, f32[8,3,256]{2,1,0:T(4,128)S(1)}, f32[8,256]{1,0:T(8,128)S(1)}, f32[8,256]{1,0:T(8,128)S(1)}, f32[8,256]{1,0:T(8,128)S(1)}, /*inde...) while((s32[]{:T(128)}, f32[8,3,256]{2,1,0:T(4,128)S(1)}, ...), condition=%wide.region_11.11_spmd, body=%wide.region_7.10_spmd.sunk | while | flops 3865858 | bytes 1648833 | solution.py:148
  190.0 8.7 %while.112 = (s32[]{:T(128)}, f32[8,3,256]{2,1,0:T(4,128)S(1)}, f32[8,256]{1,0:T(8,128)S(1)}, f32[8,256]{1,0:T(8,128)S(1)}, f32[8,256]{1,0:T(8,128)S(1)}, /*inde...) while((s32[]{:T(128)}, f32[8,3,256]{2,1,0:T(4,128)S(1)}, ...), condition=%wide.region_11.11_spmd, body=%wide.region_7.10_spmd.sunk | while | flops 3865858 | bytes 1648833 | solution.py:148
  199.1 8.7 %while.112 = (s32[]{:T(128)}, f32[8,3,256]{2,1,0:T(4,128)S(1)}, f32[8,256]{1,0:T(8,128)S(1)}, f32[8,256]{1,0:T(8,128)S(1)}, f32[8,256]{1,0:T(8,128)S(1)}, /*inde...) while((s32[]{:T(128)}, f32[8,3,256]{2,1,0:T(4,128)S(1)}, ...), condition=%wide.region_11.11_spmd, body=%wide.region_7.10_spmd.sunk | while | flops 3865858 | bytes 1648833 | solution.py:148
  208.3 8.7 %while.112 = (s32[]{:T(128)}, f32[8,3,256]{2,1,0:T(4,128)S(1)}, f32[8,256]{1,0:T(8,128)S(1)}, f32[8,256]{1,0:T(8,128)S(1)}, f32[8,256]{1,0:T(8,128)S(1)}, /*inde...) while((s32[]{:T(128)}, f32[8,3,256]{2,1,0:T(4,128)S(1)}, ...), condition=%wide.region_11.11_spmd, body=%wide.region_7.10_spmd.sunk | while | flops 3865858 | bytes 1648833 | solution.py:148
  217.5 8.7 %while.112 = (s32[]{:T(128)}, f32[8,3,256]{2,1,0:T(4,128)S(1)}, f32[8,256]{1,0:T(8,128)S(1)}, f32[8,256]{1,0:T(8,128)S(1)}, f32[8,256]{1,0:T(8,128)S(1)}, /*inde...) while((s32[]{:T(128)}, f32[8,3,256]{2,1,0:T(4,128)S(1)}, ...), condition=%wide.region_11.11_spmd, body=%wide.region_7.10_spmd.sunk | while | flops 3865858 | bytes 1648833 | solution.py:148
  226.6 8.7 %while.112 = (s32[]{:T(128)}, f32[8,3,256]{2,1,0:T(4,128)S(1)}, f32[8,256]{1,0:T(8,128)S(1)}, f32[8,256]{1,0:T(8,128)S(1)}, f32[8,256]{1,0:T(8,128)S(1)}, /*inde...) while((s32[]{:T(128)}, f32[8,3,256]{2,1,0:T(4,128)S(1)}, ...), condition=%wide.region_11.11_spmd, body=%wide.region_7.10_spmd.sunk | while | flops 3865858 | bytes 1648833 | solution.py:148
  235.8 8.7 %while.112 = (s32[]{:T(128)}, f32[8,3,256]{2,1,0:T(4,128)S(1)}, f32[8,256]{1,0:T(8,128)S(1)}, f32[8,256]{1,0:T(8,128)S(1)}, f32[8,256]{1,0:T(8,128)S(1)}, /*inde...) while((s32[]{:T(128)}, f32[8,3,256]{2,1,0:T(4,128)S(1)}, ...), condition=%wide.region_11.11_spmd, body=%wide.region_7.10_spmd.sunk | while | flops 3865858 | bytes 1648833 | solution.py:148
  244.9 8.7 %while.112 = (s32[]{:T(128)}, f32[8,3,256]{2,1,0:T(4,128)S(1)}, f32[8,256]{1,0:T(8,128)S(1)}, f32[8,256]{1,0:T(8,128)S(1)}, f32[8,256]{1,0:T(8,128)S(1)}, /*inde...) while((s32[]{:T(128)}, f32[8,3,256]{2,1,0:T(4,128)S(1)}, ...), condition=%wide.region_11.11_spmd, body=%wide.region_7.10_spmd.sunk | while | flops 3865858 | bytes 1648833 | solution.py:148
  254.1 8.7 %while.112 = (s32[]{:T(128)}, f32[8,3,256]{2,1,0:T(4,128)S(1)}, f32[8,256]{1,0:T(8,128)S(1)}, f32[8,256]{1,0:T(8,128)S(1)}, f32[8,256]{1,0:T(8,128)S(1)}, /*inde...) while((s32[]{:T(128)}, f32[8,3,256]{2,1,0:T(4,128)S(1)}, ...), condition=%wide.region_11.11_spmd, body=%wide.region_7.10_spmd.sunk | while | flops 3865858 | bytes 1648833 | solution.py:148
  263.3 8.7 %while.112 = (s32[]{:T(128)}, f32[8,3,256]{2,1,0:T(4,128)S(1)}, f32[8,256]{1,0:T(8,128)S(1)}, f32[8,256]{1,0:T(8,128)S(1)}, f32[8,256]{1,0:T(8,128)S(1)}, /*inde...) while((s32[]{:T(128)}, f32[8,3,256]{2,1,0:T(4,128)S(1)}, ...), condition=%wide.region_11.11_spmd, body=%wide.region_7.10_spmd.sunk | while | flops 3865858 | bytes 1648833 | solution.py:148
  272.4 8.7 %while.112 = (s32[]{:T(128)}, f32[8,3,256]{2,1,0:T(4,128)S(1)}, f32[8,256]{1,0:T(8,128)S(1)}, f32[8,256]{1,0:T(8,128)S(1)}, f32[8,256]{1,0:T(8,128)S(1)}, /*inde...) while((s32[]{:T(128)}, f32[8,3,256]{2,1,0:T(4,128)S(1)}, ...), condition=%wide.region_11.11_spmd, body=%wide.region_7.10_spmd.sunk | while | flops 3865858 | bytes 1648833 | solution.py:148
  281.6 8.7 %while.112 = (s32[]{:T(128)}, f32[8,3,256]{2,1,0:T(4,128)S(1)}, f32[8,256]{1,0:T(8,128)S(1)}, f32[8,256]{1,0:T(8,128)S(1)}, f32[8,256]{1,0:T(8,128)S(1)}, /*inde...) while((s32[]{:T(128)}, f32[8,3,256]{2,1,0:T(4,128)S(1)}, ...), condition=%wide.region_11.11_spmd, body=%wide.region_7.10_spmd.sunk | while | flops 3865858 | bytes 1648833 | solution.py:148
  290.8 8.7 %while.112 = (s32[]{:T(128)}, f32[8,3,256]{2,1,0:T(4,128)S(1)}, f32[8,256]{1,0:T(8,128)S(1)}, f32[8,256]{1,0:T(8,128)S(1)}, f32[8,256]{1,0:T(8,128)S(1)}, /*inde...) while((s32[]{:T(128)}, f32[8,3,256]{2,1,0:T(4,128)S(1)}, ...), condition=%wide.region_11.11_spmd, body=%wide.region_7.10_spmd.sunk | while | flops 3865858 | bytes 1648833 | solution.py:148
  299.9 8.7 %while.112 = (s32[]{:T(128)}, f32[8,3,256]{2,1,0:T(4,128)S(1)}, f32[8,256]{1,0:T(8,128)S(1)}, f32[8,256]{1,0:T(8,128)S(1)}, f32[8,256]{1,0:T(8,128)S(1)}, /*inde...) while((s32[]{:T(128)}, f32[8,3,256]{2,1,0:T(4,128)S(1)}, ...), condition=%wide.region_11.11_spmd, body=%wide.region_7.10_spmd.sunk | while | flops 3865858 | bytes 1648833 | solution.py:148
  309.1 8.7 %while.112 = (s32[]{:T(128)}, f32[8,3,256]{2,1,0:T(4,128)S(1)}, f32[8,256]{1,0:T(8,128)S(1)}, f32[8,256]{1,0:T(8,128)S(1)}, f32[8,256]{1,0:T(8,128)S(1)}, /*inde...) while((s32[]{:T(128)}, f32[8,3,256]{2,1,0:T(4,128)S(1)}, ...), condition=%wide.region_11.11_spmd, body=%wide.region_7.10_spmd.sunk | while | flops 3865858 | bytes 1648833 | solution.py:148
  318.3 8.7 %while.112 = (s32[]{:T(128)}, f32[8,3,256]{2,1,0:T(4,128)S(1)}, f32[8,256]{1,0:T(8,128)S(1)}, f32[8,256]{1,0:T(8,128)S(1)}, f32[8,256]{1,0:T(8,128)S(1)}, /*inde...) while((s32[]{:T(128)}, f32[8,3,256]{2,1,0:T(4,128)S(1)}, ...), condition=%wide.region_11.11_spmd, body=%wide.region_7.10_spmd.sunk | while | flops 3865858 | bytes 1648833 | solution.py:148
  327.4 8.7 %while.112 = (s32[]{:T(128)}, f32[8,3,256]{2,1,0:T(4,128)S(1)}, f32[8,256]{1,0:T(8,128)S(1)}, f32[8,256]{1,0:T(8,128)S(1)}, f32[8,256]{1,0:T(8,128)S(1)}, /*inde...) while((s32[]{:T(128)}, f32[8,3,256]{2,1,0:T(4,128)S(1)}, ...), condition=%wide.region_11.11_spmd, body=%wide.region_7.10_spmd.sunk | while | flops 3865858 | bytes 1648833 | solution.py:148
  336.6 8.7 %while.112 = (s32[]{:T(128)}, f32[8,3,256]{2,1,0:T(4,128)S(1)}, f32[8,256]{1,0:T(8,128)S(1)}, f32[8,256]{1,0:T(8,128)S(1)}, f32[8,256]{1,0:T(8,128)S(1)}, /*inde...) while((s32[]{:T(128)}, f32[8,3,256]{2,1,0:T(4,128)S(1)}, ...), condition=%wide.region_11.11_spmd, body=%wide.region_7.10_spmd.sunk | while | flops 3865858 | bytes 1648833 | solution.py:148
  345.7 8.7 %while.112 = (s32[]{:T(128)}, f32[8,3,256]{2,1,0:T(4,128)S(1)}, f32[8,256]{1,0:T(8,128)S(1)}, f32[8,256]{1,0:T(8,128)S(1)}, f32[8,256]{1,0:T(8,128)S(1)}, /*inde...) while((s32[]{:T(128)}, f32[8,3,256]{2,1,0:T(4,128)S(1)}, ...), condition=%wide.region_11.11_spmd, body=%wide.region_7.10_spmd.sunk | while | flops 3865858 | bytes 1648833 | solution.py:148
  354.9 8.7 %while.112 = (s32[]{:T(128)}, f32[8,3,256]{2,1,0:T(4,128)S(1)}, f32[8,256]{1,0:T(8,128)S(1)}, f32[8,256]{1,0:T(8,128)S(1)}, f32[8,256]{1,0:T(8,128)S(1)}, /*inde...) while((s32[]{:T(128)}, f32[8,3,256]{2,1,0:T(4,128)S(1)}, ...), condition=%wide.region_11.11_spmd, body=%wide.region_7.10_spmd.sunk | while | flops 3865858 | bytes 1648833 | solution.py:148
  364.1 8.7 %while.112 = (s32[]{:T(128)}, f32[8,3,256]{2,1,0:T(4,128)S(1)}, f32[8,256]{1,0:T(8,128)S(1)}, f32[8,256]{1,0:T(8,128)S(1)}, f32[8,256]{1,0:T(8,128)S(1)}, /*inde...) while((s32[]{:T(128)}, f32[8,3,256]{2,1,0:T(4,128)S(1)}, ...), condition=%wide.region_11.11_spmd, body=%wide.region_7.10_spmd.sunk | while | flops 3865858 | bytes 1648833 | solution.py:148
  373.2 8.7 %while.112 = (s32[]{:T(128)}, f32[8,3,256]{2,1,0:T(4,128)S(1)}, f32[8,256]{1,0:T(8,128)S(1)}, f32[8,256]{1,0:T(8,128)S(1)}, f32[8,256]{1,0:T(8,128)S(1)}, /*inde...) while((s32[]{:T(128)}, f32[8,3,256]{2,1,0:T(4,128)S(1)}, ...), condition=%wide.region_11.11_spmd, body=%wide.region_7.10_spmd.sunk | while | flops 3865858 | bytes 1648833 | solution.py:148
  382.4 8.7 %while.112 = (s32[]{:T(128)}, f32[8,3,256]{2,1,0:T(4,128)S(1)}, f32[8,256]{1,0:T(8,128)S(1)}, f32[8,256]{1,0:T(8,128)S(1)}, f32[8,256]{1,0:T(8,128)S(1)}, /*inde...) while((s32[]{:T(128)}, f32[8,3,256]{2,1,0:T(4,128)S(1)}, ...), condition=%wide.region_11.11_spmd, body=%wide.region_7.10_spmd.sunk | while | flops 3865858 | bytes 1648833 | solution.py:148
  391.6 8.7 %while.112 = (s32[]{:T(128)}, f32[8,3,256]{2,1,0:T(4,128)S(1)}, f32[8,256]{1,0:T(8,128)S(1)}, f32[8,256]{1,0:T(8,128)S(1)}, f32[8,256]{1,0:T(8,128)S(1)}, /*inde...) while((s32[]{:T(128)}, f32[8,3,256]{2,1,0:T(4,128)S(1)}, ...), condition=%wide.region_11.11_spmd, body=%wide.region_7.10_spmd.sunk | while | flops 3865858 | bytes 1648833 | solution.py:148
  400.7 8.7 %while.112 = (s32[]{:T(128)}, f32[8,3,256]{2,1,0:T(4,128)S(1)}, f32[8,256]{1,0:T(8,128)S(1)}, f32[8,256]{1,0:T(8,128)S(1)}, f32[8,256]{1,0:T(8,128)S(1)}, /*inde...) while((s32[]{:T(128)}, f32[8,3,256]{2,1,0:T(4,128)S(1)}, ...), condition=%wide.region_11.11_spmd, body=%wide.region_7.10_spmd.sunk | while | flops 3865858 | bytes 1648833 | solution.py:148
  (3786 shorter events, 358.6 us)
Async XLA Ops:
  2.2 4.2 %copy-start = (f32[3,2,2,2,256]{4,3,2,1,0:T(2,128)S(1)}, f32[3,2,2,2,256]{4,3,2,1,0:T(2,128)}, u32[]{:S(2)}) copy-start(f32[3,2,2,2,256]{4,3,2,1,0:T(2,128)} %param.13) | copy-start | bytes 73732
  2.2 4.2 %copy-start.1 = (f32[3,2,2,2,256]{4,3,2,1,0:T(2,128)S(1)}, f32[3,2,2,2,256]{4,3,2,1,0:T(2,128)}, u32[]{:S(2)}) copy-start(f32[3,2,2,2,256]{4,3,2,1,0:T(2,128)} %param.14) | copy-start | bytes 73732
  2.2 4.0 collective-permute-start
  2.8 3.6 collective-permute-start.1
  6.5 6.6 %collective-permute-start.2 = (f32[7,4,1,2,256]{4,3,2,1,0:T(2,128)S(1)}, f32[7,4,1,2,256]{4,3,2,1,0:T(2,128)S(1)}, u32[]{:S(2)}, u32[]{:S(2)}) collective-permute-start(f32[7,4,1,2,256]{4,3,2,1,0:T(2,128)S(1)} %get-tuple-element.827), channel_id=1, source_target_pairs={{0,2},{2,4},{4,6},{6,0},{1,3},{3,5},{5,7},{7,1},{8,10},{10,12},{12... | collective-permute-start | bytes 172040 | tf_op jit(solution)/shard_map/ppermute | solution.py:21
  8.8 5.9 %collective-permute-start.3 = (f32[7,4,1,2,256]{4,3,2,1,0:T(2,128)S(1)}, f32[7,4,1,2,256]{4,3,2,1,0:T(2,128)S(1)}, u32[]{:S(2)}, u32[]{:S(2)}) collective-permute-start(f32[7,4,1,2,256]{4,3,2,1,0:T(2,128)S(1)} %get-tuple-element.828), channel_id=1, source_target_pairs={{2,0},{4,2},{6,4},{0,6},{3,1},{5,3},{7,5},{1,7},{10,8},{12,10},{14... | collective-permute-start | bytes 172040 | tf_op jit(solution)/shard_map/ppermute | solution.py:24
  15.0 6.1 %collective-permute-start.4 = (f32[7,4,4,1,256]{4,3,2,1,0:T(1,128)S(1)}, f32[7,4,4,1,256]{4,3,2,1,0:T(1,128)S(1)}, u32[]{:S(2)}, u32[]{:S(2)}) collective-permute-start(f32[7,4,4,1,256]{4,3,2,1,0:T(1,128)S(1)} %get-tuple-element.822), channel_id=1, source_target_pairs={{0,1},{1,0},{2,3},{3,2},{4,5},{5,4},{6,7},{7,6},{8,9},{9,8},{10,11... | collective-permute-start | bytes 344072 | tf_op jit(solution)/shard_map/ppermute | solution.py:21
  16.4 6.4 %collective-permute-start.5 = (f32[7,4,4,1,256]{4,3,2,1,0:T(1,128)S(1)}, f32[7,4,4,1,256]{4,3,2,1,0:T(1,128)S(1)}, u32[]{:S(2)}, u32[]{:S(2)}) collective-permute-start(f32[7,4,4,1,256]{4,3,2,1,0:T(1,128)S(1)} %get-tuple-element.823), channel_id=1, source_target_pairs={{1,0},{0,1},{3,2},{2,3},{5,4},{4,5},{7,6},{6,7},{9,8},{8,9},{11,10... | collective-permute-start | bytes 344072 | tf_op jit(solution)/shard_map/ppermute | solution.py:24
  17.1 0.7 copy-start.2
  17.1 0.8 copy-start.3
  147.3 3.2 collective-permute-start.6
  147.4 3.1 collective-permute-start.7
  150.6 5.7 %collective-permute-start.8 = (f32[3,4,1,2,256]{4,3,2,1,0:T(2,128)S(1)}, f32[3,4,1,2,256]{4,3,2,1,0:T(2,128)S(1)}, u32[]{:S(2)}, u32[]{:S(2)}) collective-permute-start(f32[3,4,1,2,256]{4,3,2,1,0:T(2,128)S(1)} %get-tuple-element.833), channel_id=1, source_target_pairs={{0,2},{2,4},{4,6},{6,0},{1,3},{3,5},{5,7},{7,1},{8,10},{10,12},{12... | collective-permute-start | bytes 73736 | tf_op jit(solution)/shard_map/ppermute | solution.py:21
  151.6 4.7 %collective-permute-start.9 = (f32[3,4,1,2,256]{4,3,2,1,0:T(2,128)S(1)}, f32[3,4,1,2,256]{4,3,2,1,0:T(2,128)S(1)}, u32[]{:S(2)}, u32[]{:S(2)}) collective-permute-start(f32[3,4,1,2,256]{4,3,2,1,0:T(2,128)S(1)} %get-tuple-element.834), channel_id=1, source_target_pairs={{2,0},{4,2},{6,4},{0,6},{3,1},{5,3},{7,5},{1,7},{10,8},{12,10},{14... | collective-permute-start | bytes 73736 | tf_op jit(solution)/shard_map/ppermute | solution.py:24
  156.4 4.6 %collective-permute-start.10 = (f32[3,4,4,1,256]{4,3,2,1,0:T(1,128)S(1)}, f32[3,4,4,1,256]{4,3,2,1,0:T(1,128)S(1)}, u32[]{:S(2)}, u32[]{:S(2)}) collective-permute-start(f32[3,4,4,1,256]{4,3,2,1,0:T(1,128)S(1)} %get-tuple-element.829), channel_id=1, source_target_pairs={{0,1},{1,0},{2,3},{3,2},{4,5},{5,4},{6,7},{7,6},{8,9},{9,8},{10,11... | collective-permute-start | bytes 147464 | tf_op jit(solution)/shard_map/ppermute | solution.py:21
  157.9 4.1 collective-permute-start.11
where the time goes:
time: 410 us
  other arithmetic  311 us (76%)
  local copies, waits for them, and re-layouts  33 us (8%)
  loops' own time  32.5 us (8%)
  starting transfers between devices  16.8 us (4%)
  waiting for transfers between devices  16.2 us (4%)
    mul x216, other arithmetic, force_one_cell(): other_weight[None, :]  76.2 us
    reduce_sum x216, other arithmetic, force_one_cell(): return jnp.sum(factor[None] * between, 2)  69.1 us
    reduce_sum x216, other arithmetic, force_one_cell(): jnp.sum((mine_vel[:, :, None] - other_vel[:, None, :]) * between, 0)  59.3 us
    reduce_sum x216, other arithmetic, density_one_cell(): return jnp.sum(far_weight[None, :] * kernel_value(radius_sq), 1)  58.3 us
    reduce_sum x216, other arithmetic, density_one_cell(): radius_sq = jnp.sum(between * between, 0)  37.9 us
    another operation x27, loops' own time, force_add_cells(): return running - lax.map(force_one_cell, items)  15.4 us
    ppermute x6, waiting for transfers between devices, with_halo(): lax.ppermute(lax.slice_in_dim(block, block.shape[dim] - width, None, axis...  11.9 us
    ppermute x6, starting transfers between devices, with_halo(): lax.ppermute(lax.slice_in_dim(block, 0, width, axis=dim), axis, backward)  10.1 us
  transfers between devices with their start and end apart: 12, of which 10 were waited for; matrix products, arithmetic and copies ran while one was open for 0% of the time, Pallas kernels for 0%

commit v1 on v0

v1 whole, which is shorter than its diff:
```python
import functools
import itertools
import math

import jax
import jax.numpy as jnp
import numpy as np
from jax import lax
from jax.experimental import pallas as pl
from jax.experimental.pallas import tpu as pltpu
from jax.sharding import PartitionSpec as P


SIGMA = 8.0 / math.pi
GAMMA = 5.0 / 3.0
SOFTEN = 0.01
TINY = 1e-24
LANES = 128
LANE_BITS = 7
ROWS = 64
CHUNKS = 2
SHARES = ((0, 1), (1, 2), (2, 8))
VMEM = pl.BlockSpec(memory_space=pltpu.VMEM)
SMEM = pl.BlockSpec(memory_space=pltpu.SMEM)
PARAMS = pltpu.CompilerParams(vmem_limit_bytes=24 << 20)


def shifted(size, step):
    return [(i, (i + step) % size) for i in range(size)]


def with_halo(block, sides):
    for axis, dim in sides:
        count = lax.axis_size(axis)
        size = block.shape[dim]
        if count == 2 and size == 2:
            other = lax.ppermute(block, axis, shifted(2, 1))
            low = lax.slice_in_dim(other, size - 1, None, axis=dim)
            high = lax.slice_in_dim(other, 0, 1, axis=dim)
        else:
            last = lax.slice_in_dim(block, size - 1, None, axis=dim)
            first = lax.slice_in_dim(block, 0, 1, axis=dim)
            low = lax.ppermute(last, axis, shifted(count, 1))
            high = lax.ppermute(first, axis, shifted(count, -1))
        if dim == sides[-1][1]:
            return [block, low, high]
        block = jnp.concatenate([low, block, high], axis=dim)


def halo_cells(sizes):
    wide = tuple(size + 2 for size in sizes)
    found = []
    for cell in itertools.product(*(range(size) for size in wide)):
        away = tuple(
            -1 if c == 0 else (1 if c == size + 1 else 0) for c, size in zip(cell, sizes)
        )
        if away == (0, 0, 0):
            continue
        index = (cell[0] * wide[1] + cell[1]) * wide[2] + cell[2]
        operand = {0: 0, -1: 1, 1: 2}[away[1]]
        within = cell[1] - 1 if away[1] == 0 else 0
        found.append((operand, (cell[0], within, cell[2]), index, away))
    return found


def halo_table(sizes):
    wide = tuple(size + 2 for size in sizes)
    table = []
    for own in itertools.product(*(range(size) for size in sizes)):
        line = []
        for step in itertools.product(range(3), repeat=3):
            cell = tuple(o + s for o, s in zip(own, step))
            if not all(1 <= c <= size for c, size in zip(cell, sizes)):
                line.append((cell[0] * wide[1] + cell[1]) * wide[2] + cell[2])
        table.append(line)
    assert all(len(line) == len(table[0]) for line in table)
    return np.array(table, np.int32)


def fill_list(cells, sources, lists, fills, group=CHUNKS):
    lane = lax.broadcasted_iota(jnp.int32, (8, LANES), 1)
    filled = jnp.int32(0)
    held = [jnp.full((8, LANES), fill, jnp.float32) for fill in fills]
    for cell, count in cells:
        base = lax.shift_right_logical(filled, LANE_BITS)
        shift = filled & (LANES - 1)
        keep = lane < shift
        filled = filled + count
        ahead = lax.shift_right_logical(filled, LANE_BITS) - base
        for number, (source, packed, fill) in enumerate(zip(sources, lists, fills)):
            slots = source.shape[-1]
            parts = [source[cell, :, pl.ds(at, LANES)] for at in range(0, slots, LANES)]
            parts = [pltpu.roll(part, shift, 1) for part in parts]
            edges = [held[number]] + parts + [fill]
            chunks = [jnp.where(keep, a, b) for a, b in zip(edges[:-1], edges[1:])]
            for at, chunk in enumerate(chunks):
                packed[base + at] = chunk
            held[number] = chunks[-1]
            for at in range(len(chunks) - 2, -1, -1):
                held[number] = jnp.where(ahead == at, chunks[at], held[number])
    end = lax.shift_right_logical(filled + LANES - 1, LANE_BITS)
    for packed, fill in zip(lists, fills):
        for at in range(group):
            packed[end + at] = jnp.full((8, LANES), fill, jnp.float32)
    return lax.div(end + group - 1, group)


def list_scratch(cells, slots):
    return pltpu.VMEM((cells * slots // LANES + 2 + CHUNKS, 8, LANES), jnp.float32)


def spread(tile, numbers, spread_ref, first=0):
    columns = jnp.transpose(tile)
    for at, n in enumerate(numbers):
        spread_ref[first + at] = jnp.broadcast_to(columns[:, n : n + 1], spread_ref.shape[1:])


def spread_chunk(tile, numbers, spread_ref, chunk, first=0):
    columns = jnp.transpose(tile)
    for at, n in enumerate(numbers):
        spread_ref[first + at, chunk] = jnp.broadcast_to(
            columns[:, n : n + 1], spread_ref.shape[2:]
        )


def lane_sums(values):
    return jnp.sum(jnp.transpose(values), axis=0, keepdims=True)


def separation(place, far):
    apart = [a - b for a, b in zip(place, far)]
    return apart, apart[0] * apart[0] + apart[1] * apart[1] + apart[2] * apart[2]


def kernel_value(radius_sq):
    radius_sq = jnp.maximum(radius_sq, TINY)
    outer = jnp.maximum(1.0 - radius_sq * lax.rsqrt(radius_sq), 0.0)
    twice = outer + outer
    inner = jnp.maximum(twice - 1.0, 0.0)
    return twice * outer * outer - inner * inner * inner


def pair_force(mine, far):
    apart, radius_sq = separation(mine[:3], far[:3])
    speed = [a - b for a, b in zip(mine[3:6], far[3:6])]
    closing = apart[0] * speed[0] + apart[1] * speed[1] + apart[2] * speed[2]
    closing = jnp.minimum(closing, 0.0)
    approach = closing / (radius_sq + SOFTEN)
    viscous = approach * (approach - (mine[7] + far[7])) / (mine[6] + far[6])
    radius_sq = jnp.maximum(radius_sq, TINY)
    inverse = lax.rsqrt(radius_sq)
    radius = radius_sq * inverse
    outer = jnp.maximum(1.0 - radius, 0.0)
    slope = jnp.where(radius < 0.5, 2.0 - 3.0 * radius, outer * outer * inverse)
    return slope * (mine[8] + far[8] + viscous), apart


def density_of(count, steps, list_ref, spread_ref, sum_ref):
    def one_group(group, carry):
        start = pl.multiple_of(group * ROWS, ROWS)

        def one_step(step, total):
            place = [spread_ref[n, pl.ds(start, ROWS), :] for n in range(3)]
            for at in range(CHUNKS):
                chunk = step * CHUNKS + at
                far = [list_ref[chunk, pl.ds(n, 1), :] for n in range(3)]
                weight = list_ref[chunk, pl.ds(6, 1), :]
                total = total + weight * kernel_value(separation(place, far)[1])
            return total

        total = lax.fori_loop(0, steps, one_step, jnp.zeros((ROWS, LANES), jnp.float32))
        sum_ref[pl.ds(start, ROWS), :] = total
        return carry

    lax.fori_loop(0, lax.div(count + ROWS - 1, ROWS), one_group, 0)
    slot = lax.broadcasted_iota(jnp.int32, (1, sum_ref.shape[0]), 1)
    return jnp.where(slot < count, SIGMA * lane_sums(sum_ref[...]), 0.0)


def force_of(count, steps, list_ref, state_list_ref, spread_ref, sum_ref):
    def one_group(group, carry):
        start = pl.multiple_of(group * ROWS, ROWS)

        def one_step(step, total):
            mine = [spread_ref[n, pl.ds(start, ROWS), :] for n in range(9)]
            for at in range(CHUNKS):
                chunk = step * CHUNKS + at
                far = [list_ref[chunk, pl.ds(n, 1), :] for n in range(6)]
                far += [state_list_ref[chunk, pl.ds(n, 1), :] for n in range(3)]
                factor, apart = pair_force(mine, far)
                factor = list_ref[chunk, pl.ds(6, 1), :] * factor
                total = tuple(t + factor * a for t, a in zip(total, apart))
            return total

        zero = jnp.zeros((ROWS, LANES), jnp.float32)
        total = lax.fori_loop(0, steps, one_step, (zero, zero, zero))
        for n in range(3):
            sum_ref[n, pl.ds(start, ROWS), :] = total[n]
        return carry

    lax.fori_loop(0, lax.div(count + ROWS - 1, ROWS), one_group, 0)
    slot = lax.broadcasted_iota(jnp.int32, (1, sum_ref.shape[1]), 1)
    return [
        jnp.where(slot < count, 6.0 * SIGMA * lane_sums(sum_ref[n]), 0.0) for n in range(3)
    ]


def folded(values):
    return jnp.sum(values.reshape(-1, 8, values.shape[-1]), axis=0)


def rows_of(chunks, share):
    first, last = share
    return lax.div(chunks * first + 7, 8), lax.div(chunks * last + 7, 8)


def pairs_within(chunks, rows, outputs, pair, sum_ref, fold_ref):
    span = fold_ref.shape[1]
    for n in range(outputs):
        fold_ref[n] = jnp.zeros(fold_ref.shape[1:], jnp.float32)

    def one_row(row, carry):
        def one_chunk(chunk, total):
            by_row, by_column = pair(row, chunk, True)
            for n in range(outputs):
                fold_ref[n, chunk] = fold_ref[n, chunk] + folded(by_column[n])
            return tuple(t + v for t, v in zip(total, by_row))

        total = lax.fori_loop(row + 1, chunks, one_chunk, tuple(pair(row, row, False)[0]))
        for n in range(outputs):
            sum_ref[n, row] = total[n]
        return carry

    lax.fori_loop(*rows, one_row, 0)

    def one_turn(number, carry):
        for at in range(2):
            row = rows[0] + number * 2 + at
            valid = row < rows[1]
            row = jnp.minimum(row, span - 1)
            for n in range(outputs):
                sums = folded(jnp.transpose(sum_ref[n, row]))
                fold_ref[n, row] = fold_ref[n, row] + jnp.where(valid, sums, 0.0)
        return carry

    lax.fori_loop(0, (rows[1] - rows[0] + 1) // 2, one_turn, 0)


def unpacked(fold_ref, number, filled, count, slots):
    lane = lax.broadcasted_iota(jnp.int32, (8, LANES), 1)
    base = lax.shift_right_logical(filled, LANE_BITS)
    back = LANES - (filled & (LANES - 1))
    turned = [
        pltpu.roll(fold_ref[number, base + at], back & (LANES - 1), 1) for at in range(slots // LANES + 1)
    ]
    parts = [jnp.where(lane < back, a, b) for a, b in zip(turned[:-1], turned[1:])]
    row = jnp.sum(jnp.concatenate(parts, axis=1), axis=0, keepdims=True)
    slot = lax.broadcasted_iota(jnp.int32, (1, slots), 1)
    return jnp.where(slot < count, row, 0.0)


def cell_place(target, sizes):
    target = jnp.asarray(target, jnp.int32)
    _, size_y, size_z = sizes
    along = lax.div(target, size_z)
    return lax.div(along, size_y), lax.rem(along, size_y), lax.rem(target, size_z)


def own_place(target, sizes):
    along_x, along_y, along_z = cell_place(target, sizes)
    return along_x, along_y, pl.ds(along_z, 1), slice(None)


def state_tile(density, entropy):
    density = jnp.broadcast_to(density, (8, density.shape[-1]))
    entropy = jnp.broadcast_to(entropy, (8, entropy.shape[-1]))
    active = entropy > 0.0
    safe = jnp.where(active, density, 1.0)
    third = jnp.exp(jnp.log(safe) * (1.0 / 3.0))
    sound = jnp.sqrt(GAMMA * entropy) * third
    row = lax.broadcasted_iota(jnp.int32, safe.shape, 0)
    tile = jnp.where(row == 0, 0.25 * safe, jnp.where(row == 1, 0.25 * sound, entropy / third))
    return tile


def pack_kernel(
    count_hbm, position_hbm, velocity_hbm, mass_hbm, entropy_hbm, out_ref,
    count_ref, position_ref, velocity_ref, mass_ref, entropy_ref, sems,
):
    sources = (count_hbm, position_hbm, velocity_hbm, mass_hbm, entropy_hbm)
    targets = (count_ref, position_ref, velocity_ref, mass_ref, entropy_ref)
    copies = [
        pltpu.make_async_copy(source, target, sems.at[n])
        for n, (source, target) in enumerate(zip(sources, targets))
    ]
    for copy in copies:
        copy.start()
    for copy in copies:
        copy.wait()
    slots = mass_ref.shape[-1]
    slot = lax.broadcasted_iota(jnp.int32, (8, slots), 1)
    for place in np.ndindex(mass_ref.shape[:3]):
        at = place[:2] + (pl.ds(place[2], 1), slice(None))
        rows = [position_ref[n, *at] + float(place[n]) for n in range(3)]
        rows += [velocity_ref[n, *at] for n in range(3)]
        rows += [mass_ref[at], entropy_ref[at]]
        tile = jnp.concatenate(rows, axis=0)
        out_ref[place] = jnp.where(slot < count_ref[place], tile, 0.0)


def density_own(count_ref, own_ref, out_ref, list_ref, spread_ref, sum_ref, fold_ref, *, share):
    _, _, slots = own_ref.shape
    counts = [count_ref[p] for p in np.ndindex(count_ref.shape)]
    chunks = fill_list(list(enumerate(counts)), [own_ref], [list_ref], [0.0], 1)

    def one_spread(chunk, carry):
        spread_chunk(list_ref[chunk], (0, 1, 2, 6), spread_ref, chunk)
        return carry

    rows = rows_of(chunks, share)
    lax.fori_loop(*rows, one_spread, 0)

    def pair(row, chunk, both):
        mine = [spread_ref[n, row] for n in range(4)]
        far = [list_ref[chunk, pl.ds(n, 1), :] for n in range(3)]
        value = kernel_value(separation(mine[:3], far)[1])
        weight = list_ref[chunk, pl.ds(6, 1), :]
        return [weight * value], [mine[3] * value] if both else None

    pairs_within(chunks, rows, 1, pair, sum_ref, fold_ref)
    filled = jnp.int32(0)
    for cell, count in enumerate(counts):
        out_ref[pl.ds(cell, 1), :] = SIGMA * unpacked(fold_ref, 0, filled, count, slots)
        filled = filled + count


def density_halo(
    count_ref, table_ref, own_ref, *refs, sizes, parts
):
    partial_refs, piece_refs = refs[:parts], refs[parts : parts + 3]
    rho_ref, again_ref, grid_ref, grid_count_ref, lists_ref, spread_ref, sum_ref = refs[
        parts + 3 :
    ]
    slots = own_ref.shape[-1]
    row = lax.broadcasted_iota(jnp.int32, (8, slots), 0)
    for operand, cell, index, away in halo_cells(sizes):
        tile = piece_refs[operand][cell[0], cell[1], cell[2]]
        grid_count_ref[index] = jnp.sum((tile[7:8] > 0.0).astype(jnp.int32))
        for dim in range(3):
            if away[dim]:
                tile = tile + jnp.where(row == dim, float(away[dim] * sizes[dim]), 0.0)
        grid_ref[index] = tile

    def one_target(target):
        cells = [table_ref[target, n] for n in range(table_ref.shape[1])]
        list_ref = lists_ref.at[target]
        steps = fill_list(
            [(c, grid_count_ref[c]) for c in cells], [grid_ref], [list_ref], [0.0]
        )
        spread(own_ref[target], range(3), spread_ref)
        return density_of(count_ref[*cell_place(target, sizes)], steps, list_ref, spread_ref, sum_ref)

    def one(target, carry):
        total = one_target(target)
        for partial_ref in partial_refs:
            total = total + partial_ref[pl.ds(target, 1), :]
        rho_ref[*own_place(target, sizes)] = total
        again_ref[*own_place(target, sizes)] = total
        return carry

    lax.fori_loop(0, own_ref.shape[0], one, 0)


def force_own(
    count_ref, own_ref, rho_ref, out_ref,
    list_ref, state_ref, state_list_ref, spread_ref, sum_ref, fold_ref, *, share,
):
    cells, _, slots = own_ref.shape
    counts = [count_ref[p] for p in np.ndindex(count_ref.shape)]
    for cell in range(cells):
        density = rho_ref[*own_place(cell, rho_ref.shape[:3])]
        state_ref[cell] = state_tile(density, own_ref[cell, pl.ds(7, 1), :])
    chunks = fill_list(
        list(enumerate(counts)), [own_ref, state_ref], [list_ref, state_list_ref], [0.0, 1.0], 1
    )

    def one_spread(chunk, carry):
        spread_chunk(list_ref[chunk], range(7), spread_ref, chunk)
        spread_chunk(state_list_ref[chunk], range(3), spread_ref, chunk, 7)
        return carry

    rows = rows_of(chunks, share)
    lax.fori_loop(*rows, one_spread, 0)

    def pair(row, chunk, both):
        mine = [spread_ref[n, row] for n in (0, 1, 2, 3, 4, 5, 7, 8, 9)]
        far = [list_ref[chunk, pl.ds(n, 1), :] for n in range(6)]
        far += [state_list_ref[chunk, pl.ds(n, 1), :] for n in range(3)]
        factor, apart = pair_force(mine, far)
        weight = list_ref[chunk, pl.ds(6, 1), :] * factor
        by_row = [weight * a for a in apart]
        if not both:
            return by_row, None
        weight = spread_ref[6, row] * factor
        return by_row, [-(weight * a) for a in apart]

    pairs_within(chunks, rows, 3, pair, sum_ref, fold_ref)
    for n in range(3):
        filled = jnp.int32(0)
        for cell, count in enumerate(counts):
            out_ref[n, pl.ds(cell, 1), :] = (6.0 * SIGMA) * unpacked(
                fold_ref, n, filled, count, slots
            )
            filled = filled + count


def force_halo(
    count_ref, table_ref, own_ref, density_ref, grid_count_ref, grid_ref, lists_ref,
    *refs, sizes, parts,
):
    partial_refs, piece_refs = refs[:parts], refs[parts : parts + 3]
    out_ref, state_ref, state_list_ref, spread_ref, sum_ref = refs[parts + 3 :]
    for operand, cell, index, _ in halo_cells(sizes):
        density = piece_refs[operand][cell[0], cell[1], pl.ds(cell[2], 1), :]
        state_ref[index] = state_tile(density, grid_ref[index, pl.ds(7, 1), :])

    def one_target(target):
        cells = [table_ref[target, n] for n in range(table_ref.shape[1])]
        steps = fill_list(
            [(c, grid_count_ref[c]) for c in cells], [state_ref], [state_list_ref], [1.0]
        )
        spread(own_ref[target], range(6), spread_ref)
        density = density_ref[*own_place(target, sizes)]
        spread(state_tile(density, own_ref[target, pl.ds(7, 1), :]), range(3), spread_ref, 6)
        return force_of(
            count_ref[*cell_place(target, sizes)], steps, lists_ref.at[target], state_list_ref, spread_ref, sum_ref
        )

    def one(target, carry):
        sums = one_target(target)
        for n in range(3):
            total = sums[n]
            for partial_ref in partial_refs:
                total = total + partial_ref[n, pl.ds(target, 1), :]
            out_ref[n, *own_place(target, sizes)] = total
        return carry

    lax.fori_loop(0, own_ref.shape[0], one, 0)


def cost(pairs, flops):
    return pl.CostEstimate(flops=pairs * flops, transcendentals=pairs, bytes_accessed=1 << 20)


def per_device(positions, velocities, masses, entropy, counts):
    sizes = masses.shape[:3]
    slots = masses.shape[3]
    cells = sizes[0] * sizes[1] * sizes[2]
    wide = (sizes[0] + 2) * (sizes[1] + 2) * (sizes[2] + 2)
    assert all(size <= 2 for size in sizes)
    packed = pl.pallas_call(
        pack_kernel,
        out_shape=jax.ShapeDtypeStruct(sizes + (8, slots), jnp.float32),
        in_specs=[pl.BlockSpec(memory_space=pltpu.HBM)] * 5,
        out_specs=VMEM,
        scratch_shapes=[
            pltpu.SMEM(counts.shape, jnp.int32),
            pltpu.VMEM(positions.shape, jnp.float32),
            pltpu.VMEM(velocities.shape, jnp.float32),
            pltpu.VMEM(masses.shape, jnp.float32),
            pltpu.VMEM(entropy.shape, jnp.float32),
            pltpu.SemaphoreType.DMA((5,)),
        ],
        compiler_params=PARAMS,
        name="pack",
    )(counts, positions, velocities, masses, entropy)
    own = packed.reshape(cells, 8, slots)
    table = jnp.asarray(halo_table(sizes))
    near = table.shape[1]
    pairs = cells * slots * slots
    own_chunks = cells * slots // LANES + 2

    def own_rows(fields):
        return pltpu.VMEM((fields, own_chunks, LANES, LANES), jnp.float32)

    def own_folds(outputs):
        return pltpu.VMEM((outputs, own_chunks, 8, LANES), jnp.float32)

    halo_order = (("gz", 2), ("gx", 0), ("gy", 1))
    spread3 = pltpu.VMEM((3, slots, LANES), jnp.float32)
    spread9 = pltpu.VMEM((9, slots, LANES), jnp.float32)
    sums = pltpu.VMEM((slots, LANES), jnp.float32)
    three_sums = pltpu.VMEM((3, slots, LANES), jnp.float32)
    own_list = list_scratch(cells, slots)
    halo_list = list_scratch(near, slots)

    partials = [pl.pallas_call(
        functools.partial(density_own, share=share),
        out_shape=jax.ShapeDtypeStruct((cells, slots), jnp.float32),
        in_specs=[SMEM, VMEM],
        out_specs=VMEM,
        scratch_shapes=[own_list, own_rows(4), own_rows(1), own_folds(1)],
        compiler_params=PARAMS,
        cost_estimate=cost(pairs * cells, 22),
    )(counts, own) for share in SHARES]
    pieces = with_halo(packed, halo_order)
    result, density, grid, grid_counts, lists = pl.pallas_call(
        functools.partial(density_halo, sizes=sizes, parts=len(SHARES)),
        out_shape=(
            jax.ShapeDtypeStruct(masses.shape, jnp.float32),
            jax.ShapeDtypeStruct(masses.shape, jnp.float32),
            jax.ShapeDtypeStruct((wide, 8, slots), jnp.float32),
            jax.ShapeDtypeStruct((wide,), jnp.int32),
            jax.ShapeDtypeStruct((cells,) + halo_list.shape, jnp.float32),
        ),
        in_specs=[SMEM, SMEM] + [VMEM] * (4 + len(SHARES)),
        out_specs=(VMEM, VMEM, VMEM, SMEM, VMEM),
        scratch_shapes=[spread3, sums],
        compiler_params=PARAMS,
        cost_estimate=cost(pairs * near, 22),
        name="density_halo",
    )(counts, table, own, *partials, *pieces)
    partials = [pl.pallas_call(
        functools.partial(force_own, share=share),
        out_shape=jax.ShapeDtypeStruct((3, cells, slots), jnp.float32),
        in_specs=[SMEM, VMEM, VMEM],
        out_specs=VMEM,
        scratch_shapes=[
            own_list, pltpu.VMEM((cells, 8, slots), jnp.float32), own_list,
            own_rows(10), own_rows(3), own_folds(3),
        ],
        compiler_params=PARAMS,
        cost_estimate=cost(pairs * cells, 50),
    )(counts, own, density) for share in SHARES]
    pieces = with_halo(density, halo_order)
    acceleration = pl.pallas_call(
        functools.partial(force_halo, sizes=sizes, parts=len(SHARES)),
        out_shape=jax.ShapeDtypeStruct(positions.shape, jnp.float32),
        in_specs=[SMEM, SMEM, VMEM, VMEM, SMEM] + [VMEM] * (5 + len(SHARES)),
        out_specs=VMEM,
        scratch_shapes=[
            pltpu.VMEM((wide, 8, slots), jnp.float32), halo_list,
            spread9, three_sums,
        ],
        compiler_params=PARAMS,
        cost_estimate=cost(pairs * near, 50),
        name="force_halo",
    )(counts, table, own, density, grid_counts, grid, lists, *partials, *pieces)
    return (result, acceleration)


def solution(mesh):
    return jax.shard_map(
        per_device,
        mesh=mesh,
        in_specs=(
            P(None, "gx", "gy", "gz", None),
            P(None, "gx", "gy", "gz", None),
            P("gx", "gy", "gz", None),
            P("gx", "gy", "gz", None),
            P("gx", "gy", "gz"),
        ),
        out_specs=(P("gx", "gy", "gz", None), P(None, "gx", "gy", "gz", None)),
        check_vma=False,
    )
```

time: 410 us -> 107 us (0.26)
  the two profiles are of different devices: /device:TPU:0 before, /device:TPU:6 now
where the time goes in v1:
time: 107 us; the launch traced here: 106 us
  Pallas kernels  86 us (80%)
  starting transfers between devices  9.98 us (9%)
  waiting for transfers between devices  5.7 us (5%)
  local copies, waits for them, and re-layouts  3.6 us (3%)
    pallas_call x1, Pallas kernels, per_device(): pl.pallas_call(functools.partial(force_halo, sizes=sizes, parts=len(SHARE...  32.5 us
    pallas_call x3, Pallas kernels, per_device(): pl.pallas_call(functools.partial(force_own, share=share), out_shape=jax.S...  23.5 us
    pallas_call x1, Pallas kernels, per_device(): pl.pallas_call(functools.partial(density_halo, sizes=sizes, parts=len(SHA...  16.4 us
    pallas_call x3, Pallas kernels, per_device(): pl.pallas_call(functools.partial(density_own, share=share), out_shape=jax...  12.8 us
    ppermute x4, starting transfers between devices, with_halo(): high = lax.ppermute(first, axis, shifted(count, -1))  7.18 us
    ppermute x2, waiting for transfers between devices, with_halo(): other = lax.ppermute(block, axis, shifted(2, 1))  3.73 us
    unnamed x12, local copies, waits for them, and re-layouts  3.55 us
  transfers between devices with their start and end apart: 10, of which 2 were waited for; matrix products, arithmetic and copies ran while one was open for 0% of the time, Pallas kernels for 34%

profile of v1, /device:TPU:6, one launch (start us, length us, event | category | flops | bytes accessed | tf_op | source)
XLA Modules:
  0.0 106.2 jit_solution(16333205915290660462)
XLA Ops:
  0.6 0.0 copy-start
  0.6 0.7 copy-done
  1.4 0.0 copy-start.1
  1.4 0.7 copy-done.1
  2.1 0.0 copy-start.2
  2.1 0.7 copy-done.2
  2.8 0.0 copy-start.3
  2.8 0.7 copy-done.3
  3.5 0.0 copy-start.4
  3.5 0.7 copy-done.4
  4.2 0.7 pack.1
  4.8 0.6 collective-permute-start
  5.4 3.7 %collective-permute-done = f32[2,2,2,8,256]{4,3,2,1,0:T(8,128)S(1)} collective-permute-done((f32[2,2,2,8,256]{4,3,2,1,0:T(8,128)S(1)}, f32[2,2,2,8,256]{4,3,2,1,0:T(8,128)S(1)}, u32[]{:S(2)}, u32[]{:S(2)}) %collective-permute-start) | collective-permute-done | bytes 65568 | tf_op jit(solution)/shard_map/ppermute | solution.py:37
  9.2 0.1 collective-permute-start.1
  9.3 1.7 %collective-permute-start.2 = (f32[1,2,4,8,256]{4,3,2,1,0:T(8,128)S(1)}, f32[1,2,4,8,256]{4,3,2,1,0:T(8,128)S(1)}, u32[]{:S(2)}, u32[]{:S(2)}) collective-permute-start(f32[1,2,4,8,256]{4,3,2,1,0:T(8,128)S(1)} %get-tuple-element.15), channel_id=1, source_target_pairs={{0,24},{8,0},{16,8},{24,16},{1,25},{9,1},{17,9},{25,17},{2,26},{10... | collective-permute-start | bytes 196616 | tf_op jit(solution)/shard_map/ppermute | solution.py:44
  11.0 1.9 %collective-permute-done.1 = f32[1,2,4,8,256]{4,3,2,1,0:T(8,128)S(1)} collective-permute-done((f32[1,2,4,8,256]{4,3,2,1,0:T(8,128)S(1)}, f32[1,2,4,8,256]{4,3,2,1,0:T(8,128)S(1)}, u32[]{:S(2)}, u32[]{:S(2)}) %collective-permute-start.1) | collective-permute-done | bytes 65568 | tf_op jit(solution)/shard_map/ppermute | solution.py:43
  13.0 0.0 collective-permute-done.2
  13.0 3.7 %collective-permute-start.4 = (f32[4,1,4,8,256]{4,3,2,1,0:T(8,128)S(1)}, f32[4,1,4,8,256]{4,3,2,1,0:T(8,128)S(1)}, u32[]{:S(2)}, u32[]{:S(2)}) collective-permute-start(f32[4,1,4,8,256]{4,3,2,1,0:T(8,128)S(1)} %get-tuple-element.12), channel_id=1, source_target_pairs={{0,6},{2,0},{4,2},{6,4},{1,7},{3,1},{5,3},{7,5},{8,14},{10,8},{12,... | collective-permute-start | bytes 393224 | tf_op jit(solution)/shard_map/ppermute | solution.py:44
  16.7 0.0 collective-permute-start.3
  16.7 6.7 %shard_map.79.refs_2_ = f32[8,256]{1,0:T(8,128)S(1)} custom-call(s32[2,2,2]{2,1,0:T(2,128)S(1)} %copy-done.4, f32[8,8,256]{2,1,0:T(8,128)S(1)} %bitcast.1), custom_call_target="tpu_custom_call" | custom-call | flops 92274688 | bytes 1048576 | tf_op jit(solution)/shard_map/pallas_call | solution.py:497
  23.4 2.9 %shard_map.78.refs_1_ = f32[8,256]{1,0:T(8,128)S(1)} custom-call(s32[2,2,2]{2,1,0:T(2,128)S(1)} %copy-done.4, f32[8,8,256]{2,1,0:T(8,128)S(1)} %bitcast.2), custom_call_target="tpu_custom_call" | custom-call | flops 92274688 | bytes 1048576 | tf_op jit(solution)/shard_map/pallas_call | solution.py:497
  26.3 0.0 copy-start.5
  26.3 3.2 %shard_map.77.refs_0_ = f32[8,256]{1,0:T(8,128)S(1)} custom-call(s32[2,2,2]{2,1,0:T(2,128)S(1)} %copy-done.4, f32[8,8,256]{2,1,0:T(8,128)S(1)} %bitcast.3), custom_call_target="tpu_custom_call" | custom-call | flops 92274688 | bytes 1048576 | tf_op jit(solution)/shard_map/pallas_call | solution.py:497
  29.5 0.0 collective-permute-done.4.refs_5_
  29.5 0.0 collective-permute-done.3.refs_4_
  29.6 0.0 copy-done.5
  29.6 16.4 %density_halo.1 = (f32[2,2,2,256]{3,2,1,0:T(2,128)}, f32[2,2,2,256]{3,2,1,0:T(2,128)S(1)}, f32[64,8,256]{2,1,0:T(8,128)S(1)}, s32[64]{0:T(128)S(1)}, f32[8,42,8,128]{3,2,1,0:T(8,128)S(1)}) custom-call(s32[2,2,2]{2,1,0:T(2,128)S(1)} %copy-done.4, s32[8,19]{1,0:T(8,128)S(1)} %copy-done.5, f32[8,8,256]{2,1,0:T(8,128)S(1)} %bitcast.4, ...), custom_call_target="tpu_custom_call" | custom-call | flops 219152384 | bytes 1048576 | tf_op jit(solution)/shard_map/density_halo/pallas_call | solution.py:507
  46.0 0.1 collective-permute-start.5
  46.1 12.5 %shard_map.82.refs_2_ = f32[3,8,256]{2,1,0:T(8,128)S(1)} custom-call(s32[2,2,2]{2,1,0:T(2,128)S(1)} %copy-done.4, f32[8,8,256]{2,1,0:T(8,128)S(1)} %bitcast.5, f32[2,2,2,256]{3,2,1,0:T(2,128)S(1)} %get-tuple-element.8.rho_ref.density_ref), custom_call_target="tpu_custom_call" | custom-call | flops 209715200 | bytes 1048576 | tf_op jit(solution)/shard_map/pallas_call | solution.py:523
  58.5 0.0 collective-permute-done.5
  58.6 0.1 collective-permute-start.6
  58.7 1.7 %collective-permute-start.7 = (f32[1,2,4,256]{3,2,1,0:T(4,128)S(1)}, f32[1,2,4,256]{3,2,1,0:T(4,128)S(1)}, u32[]{:S(2)}, u32[]{:S(2)}) collective-permute-start(f32[1,2,4,256]{3,2,1,0:T(4,128)S(1)} %get-tuple-element.21), channel_id=1, source_target_pairs={{0,24},{8,0},{16,8},{24,16},{1,25},{9,1},{17,9},{25,17},{2,26},{10... | collective-permute-start | bytes 24584 | tf_op jit(solution)/shard_map/ppermute | solution.py:44
  60.4 5.2 %shard_map.81.refs_1_ = f32[3,8,256]{2,1,0:T(8,128)S(1)} custom-call(s32[2,2,2]{2,1,0:T(2,128)S(1)} %copy-done.4, f32[8,8,256]{2,1,0:T(8,128)S(1)} %bitcast.6, f32[2,2,2,256]{3,2,1,0:T(2,128)S(1)} %get-tuple-element.8.rho_ref.density_ref), custom_call_target="tpu_custom_call" | custom-call | flops 209715200 | bytes 1048576 | tf_op jit(solution)/shard_map/pallas_call | solution.py:523
  65.6 0.0 collective-permute-done.6
  65.6 0.0 collective-permute-done.7
  65.7 0.1 collective-permute-start.9
  65.8 2.0 %collective-permute-start.8 = (f32[4,1,4,256]{3,2,1,0:T(4,128)S(1)}, f32[4,1,4,256]{3,2,1,0:T(4,128)S(1)}, u32[]{:S(2)}, u32[]{:S(2)}) collective-permute-start(f32[4,1,4,256]{3,2,1,0:T(4,128)S(1)} %get-tuple-element.19), channel_id=1, source_target_pairs={{0,2},{2,4},{4,6},{6,0},{1,3},{3,5},{5,7},{7,1},{8,10},{10,12},{12... | collective-permute-start | bytes 49160 | tf_op jit(solution)/shard_map/ppermute | solution.py:43
  67.8 5.9 %shard_map.80.refs_0_ = f32[3,8,256]{2,1,0:T(8,128)S(1)} custom-call(s32[2,2,2]{2,1,0:T(2,128)S(1)} %copy-done.4, f32[8,8,256]{2,1,0:T(8,128)S(1)} %bitcast.7, f32[2,2,2,256]{3,2,1,0:T(2,128)S(1)} %get-tuple-element.8.rho_ref.density_ref), custom_call_target="tpu_custom_call" | custom-call | flops 209715200 | bytes 1048576 | tf_op jit(solution)/shard_map/pallas_call | solution.py:523
  73.6 0.0 collective-permute-done.9.refs_5_
  73.6 0.0 collective-permute-done.8.refs_4_
  73.7 32.5 %force_halo.1 = f32[3,2,2,2,256]{4,3,2,1,0:T(2,128)} custom-call(s32[2,2,2]{2,1,0:T(2,128)S(1)} %copy-done.4, s32[8,19]{1,0:T(8,128)S(1)} %copy-done.5, f32[8,8,256]{2,1,0:T(8,128)S(1)} %bitcast.8, f32[2,2,2,256]{3,2,1,0:T(2,128)S(1)} %get-tuple-element.8.rho_ref.density_ref, s32[64]{0:T(128)S(1)} %get-tuple-element.9.grid_count_ref, ...), custom_call_target="tpu_custom_call" | custom-call | flops 498073600 | bytes 1048576 | tf_op jit(solution)/shard_map/force_halo/pallas_call | solution.py:536
  (10 shorter events, 0.1 us)
Async XLA Ops:
  0.6 0.7 copy-start
  1.4 0.7 copy-start.1
  2.1 0.7 copy-start.2
  2.8 0.7 copy-start.3
  3.5 0.7 copy-start.4
  4.8 4.3 %collective-permute-start = (f32[2,2,2,8,256]{4,3,2,1,0:T(8,128)S(1)}, f32[2,2,2,8,256]{4,3,2,1,0:T(8,128)S(1)}, u32[]{:S(2)}, u32[]{:S(2)}) collective-permute-start(f32[2,2,2,8,256]{4,3,2,1,0:T(8,128)S(1)} %pack.1), channel_id=1, source_target_pairs={{0,1},{1,0},{2,3},{3,2},{4,5},{5,4},{6,7},{7,6},{8,9},{9,8},{10,11... | collective-permute-start | bytes 196616 | tf_op jit(solution)/shard_map/ppermute | solution.py:37
  9.2 3.7 %collective-permute-start.1 = (f32[1,2,4,8,256]{4,3,2,1,0:T(8,128)S(1)}, f32[1,2,4,8,256]{4,3,2,1,0:T(8,128)S(1)}, u32[]{:S(2)}, u32[]{:S(2)}) collective-permute-start(f32[1,2,4,8,256]{4,3,2,1,0:T(8,128)S(1)} %get-tuple-element.14), channel_id=1, source_target_pairs={{0,8},{8,16},{16,24},{24,0},{1,9},{9,17},{17,25},{25,1},{2,10},{10... | collective-permute-start | bytes 196616 | tf_op jit(solution)/shard_map/ppermute | solution.py:43
  9.3 3.7 %collective-permute-start.2 = (f32[1,2,4,8,256]{4,3,2,1,0:T(8,128)S(1)}, f32[1,2,4,8,256]{4,3,2,1,0:T(8,128)S(1)}, u32[]{:S(2)}, u32[]{:S(2)}) collective-permute-start(f32[1,2,4,8,256]{4,3,2,1,0:T(8,128)S(1)} %get-tuple-element.15), channel_id=1, source_target_pairs={{0,24},{8,0},{16,8},{24,16},{1,25},{9,1},{17,9},{25,17},{2,26},{10... | collective-permute-start | bytes 196616 | tf_op jit(solution)/shard_map/ppermute | solution.py:44
  13.0 16.5 %collective-permute-start.4 = (f32[4,1,4,8,256]{4,3,2,1,0:T(8,128)S(1)}, f32[4,1,4,8,256]{4,3,2,1,0:T(8,128)S(1)}, u32[]{:S(2)}, u32[]{:S(2)}) collective-permute-start(f32[4,1,4,8,256]{4,3,2,1,0:T(8,128)S(1)} %get-tuple-element.12), channel_id=1, source_target_pairs={{0,6},{2,0},{4,2},{6,4},{1,7},{3,1},{5,3},{7,5},{8,14},{10,8},{12,... | collective-permute-start | bytes 393224 | tf_op jit(solution)/shard_map/ppermute | solution.py:44
  16.7 12.9 %collective-permute-start.3 = (f32[4,1,4,8,256]{4,3,2,1,0:T(8,128)S(1)}, f32[4,1,4,8,256]{4,3,2,1,0:T(8,128)S(1)}, u32[]{:S(2)}, u32[]{:S(2)}) collective-permute-start(f32[4,1,4,8,256]{4,3,2,1,0:T(8,128)S(1)} %get-tuple-element.13), channel_id=1, source_target_pairs={{0,2},{2,4},{4,6},{6,0},{1,3},{3,5},{5,7},{7,1},{8,10},{10,12},{12... | collective-permute-start | bytes 393224 | tf_op jit(solution)/shard_map/ppermute | solution.py:43
  26.3 3.2 %copy-start.5 = (s32[8,19]{1,0:T(8,128)S(1)}, s32[8,19]{1,0:T(8,128)}, u32[]{:S(2)}) copy-start(s32[8,19]{1,0:T(8,128)} %constant.2.clone.table_ref) | copy-start | bytes 1828
  46.0 12.6 %collective-permute-start.5 = (f32[2,2,2,256]{3,2,1,0:T(2,128)S(1)}, f32[2,2,2,256]{3,2,1,0:T(2,128)S(1)}, u32[]{:S(2)}, u32[]{:S(2)}) collective-permute-start(f32[2,2,2,256]{3,2,1,0:T(2,128)S(1)} %get-tuple-element.8.rho_ref.density_ref), channel_id=1, source_target_pairs={{0,1},{1,0},{2,3},{3,2},{4,5},{5,4},{6,7},{7,6},{8,9},{9,8},{10,11... | collective-permute-start | bytes 24584 | tf_op jit(solution)/shard_map/ppermute | solution.py:37
  58.6 7.0 %collective-permute-start.6 = (f32[1,2,4,256]{3,2,1,0:T(4,128)S(1)}, f32[1,2,4,256]{3,2,1,0:T(4,128)S(1)}, u32[]{:S(2)}, u32[]{:S(2)}) collective-permute-start(f32[1,2,4,256]{3,2,1,0:T(4,128)S(1)} %get-tuple-element.20), channel_id=1, source_target_pairs={{0,8},{8,16},{16,24},{24,0},{1,9},{9,17},{17,25},{25,1},{2,10},{10... | collective-permute-start | bytes 24584 | tf_op jit(solution)/shard_map/ppermute | solution.py:43
  58.7 7.0 %collective-permute-start.7 = (f32[1,2,4,256]{3,2,1,0:T(4,128)S(1)}, f32[1,2,4,256]{3,2,1,0:T(4,128)S(1)}, u32[]{:S(2)}, u32[]{:S(2)}) collective-permute-start(f32[1,2,4,256]{3,2,1,0:T(4,128)S(1)} %get-tuple-element.21), channel_id=1, source_target_pairs={{0,24},{8,0},{16,8},{24,16},{1,25},{9,1},{17,9},{25,17},{2,26},{10... | collective-permute-start | bytes 24584 | tf_op jit(solution)/shard_map/ppermute | solution.py:44
  65.7 7.9 %collective-permute-start.9 = (f32[4,1,4,256]{3,2,1,0:T(4,128)S(1)}, f32[4,1,4,256]{3,2,1,0:T(4,128)S(1)}, u32[]{:S(2)}, u32[]{:S(2)}) collective-permute-start(f32[4,1,4,256]{3,2,1,0:T(4,128)S(1)} %get-tuple-element.18), channel_id=1, source_target_pairs={{0,6},{2,0},{4,2},{6,4},{1,7},{3,1},{5,3},{7,5},{8,14},{10,8},{12,... | collective-permute-start | bytes 49160 | tf_op jit(solution)/shard_map/ppermute | solution.py:44
  65.8 7.9 %collective-permute-start.8 = (f32[4,1,4,256]{3,2,1,0:T(4,128)S(1)}, f32[4,1,4,256]{3,2,1,0:T(4,128)S(1)}, u32[]{:S(2)}, u32[]{:S(2)}) collective-permute-start(f32[4,1,4,256]{3,2,1,0:T(4,128)S(1)} %get-tuple-element.19), channel_id=1, source_target_pairs={{0,2},{2,4},{4,6},{6,0},{1,3},{3,5},{5,7},{7,1},{8,10},{10,12},{12... | collective-permute-start | bytes 49160 | tf_op jit(solution)/shard_map/ppermute | solution.py:43

commit v2 on v1

--- a/solution.py
+++ b/solution.py
@@ -19,7 +19,11 @@
 LANE_BITS = 7
 ROWS = 64
 CHUNKS = 2
-SHARES = ((0, 1), (1, 2), (2, 8))
+PAD = 8
+PARTS = 16
+ORDER = (("gy", 1), ("gz", 2), ("gx", 0))
+DENSITY_SHARES = ((0, 3), (3, 6), (6, PARTS))
+FORCE_SHARES = ((0, 2), (2, 4), (4, PARTS))
 VMEM = pl.BlockSpec(memory_space=pltpu.VMEM)
 SMEM = pl.BlockSpec(memory_space=pltpu.SMEM)
 PARAMS = pltpu.CompilerParams(vmem_limit_bytes=24 << 20)
@@ -57,9 +61,10 @@
         if away == (0, 0, 0):
             continue
         index = (cell[0] * wide[1] + cell[1]) * wide[2] + cell[2]
-        operand = {0: 0, -1: 1, 1: 2}[away[1]]
-        within = cell[1] - 1 if away[1] == 0 else 0
-        found.append((operand, (cell[0], within, cell[2]), index, away))
+        last = ORDER[-1][1]
+        within = list(cell)
+        within[last] = cell[last] - 1 if away[last] == 0 else 0
+        found.append(({0: 0, -1: 1, 1: 2}[away[last]], tuple(within), index, away))
     return found
 
 
@@ -111,16 +116,35 @@
 
 def spread(tile, numbers, spread_ref, first=0):
     columns = jnp.transpose(tile)
+    rows = columns.shape[0]
     for at, n in enumerate(numbers):
-        spread_ref[first + at] = jnp.broadcast_to(columns[:, n : n + 1], spread_ref.shape[1:])
+        spread_ref[first + at, pl.ds(0, rows), :] = jnp.broadcast_to(
+            columns[:, n : n + 1], (rows, LANES)
+        )
+
+
+def rows_at(chunk):
+    return pl.ds(pl.multiple_of(chunk * LANES, LANES), LANES)
 
 
 def spread_chunk(tile, numbers, spread_ref, chunk, first=0):
     columns = jnp.transpose(tile)
     for at, n in enumerate(numbers):
-        spread_ref[first + at, chunk] = jnp.broadcast_to(
-            columns[:, n : n + 1], spread_ref.shape[2:]
+        spread_ref[first + at, rows_at(chunk), :] = jnp.broadcast_to(
+            columns[:, n : n + 1], (LANES, LANES)
         )
+
+
+def in_twos(rows, work):
+    first, last = rows
+
+    def two(number, carry):
+        row = first + 2 * number
+        work(row)
+        work(jnp.minimum(row + 1, last - 1))
+        return carry
+
+    lax.fori_loop(0, lax.div(last - first + 1, 2), two, 0)
 
 
 def lane_sums(values):
@@ -158,9 +182,9 @@
 def density_of(count, steps, list_ref, spread_ref, sum_ref):
     def one_group(group, carry):
         start = pl.multiple_of(group * ROWS, ROWS)
+        place = [spread_ref[n, pl.ds(start, ROWS), :] for n in range(3)]
 
         def one_step(step, total):
-            place = [spread_ref[n, pl.ds(start, ROWS), :] for n in range(3)]
             for at in range(CHUNKS):
                 chunk = step * CHUNKS + at
                 far = [list_ref[chunk, pl.ds(n, 1), :] for n in range(3)]
@@ -211,7 +235,7 @@
 
 def rows_of(chunks, share):
     first, last = share
-    return lax.div(chunks * first + 7, 8), lax.div(chunks * last + 7, 8)
+    return tuple(lax.div(chunks * end + PARTS - 1, PARTS) for end in (first, last))
 
 
 def pairs_within(chunks, rows, outputs, pair, sum_ref, fold_ref):
@@ -284,7 +308,7 @@
 
 
 def pack_kernel(
-    count_hbm, position_hbm, velocity_hbm, mass_hbm, entropy_hbm, out_ref,
+    count_hbm, position_hbm, velocity_hbm, mass_hbm, entropy_hbm, out_ref, count_out,
     count_ref, position_ref, velocity_ref, mass_ref, entropy_ref, sems,
 ):
     sources = (count_hbm, position_hbm, velocity_hbm, mass_hbm, entropy_hbm)
@@ -299,7 +323,8 @@
         copy.wait()
     slots = mass_ref.shape[-1]
     slot = lax.broadcasted_iota(jnp.int32, (8, slots), 1)
-    for place in np.ndindex(mass_ref.shape[:3]):
+    for cell, place in enumerate(np.ndindex(mass_ref.shape[:3])):
+        count_out[cell] = count_ref[place]
         at = place[:2] + (pl.ds(place[2], 1), slice(None))
         rows = [position_ref[n, *at] + float(place[n]) for n in range(3)]
         rows += [velocity_ref[n, *at] for n in range(3)]
@@ -309,19 +334,19 @@
 
 
 def density_own(count_ref, own_ref, out_ref, list_ref, spread_ref, sum_ref, fold_ref, *, share):
-    _, _, slots = own_ref.shape
-    counts = [count_ref[p] for p in np.ndindex(count_ref.shape)]
+    cells, _, slots = own_ref.shape
+    counts = [count_ref[c] for c in range(cells)]
     chunks = fill_list(list(enumerate(counts)), [own_ref], [list_ref], [0.0], 1)
 
-    def one_spread(chunk, carry):
+    rows = rows_of(chunks, share)
+
+    def one_spread(chunk):
         spread_chunk(list_ref[chunk], (0, 1, 2, 6), spread_ref, chunk)
-        return carry
-
-    rows = rows_of(chunks, share)
-    lax.fori_loop(*rows, one_spread, 0)
+
+    in_twos(rows, one_spread)
 
     def pair(row, chunk, both):
-        mine = [spread_ref[n, row] for n in range(4)]
+        mine = [spread_ref[n, rows_at(row), :] for n in range(4)]
         far = [list_ref[chunk, pl.ds(n, 1), :] for n in range(3)]
         value = kernel_value(separation(mine[:3], far)[1])
         weight = list_ref[chunk, pl.ds(6, 1), :]
@@ -358,7 +383,7 @@
             [(c, grid_count_ref[c]) for c in cells], [grid_ref], [list_ref], [0.0]
         )
         spread(own_ref[target], range(3), spread_ref)
-        return density_of(count_ref[*cell_place(target, sizes)], steps, list_ref, spread_ref, sum_ref)
+        return density_of(count_ref[target], steps, list_ref, spread_ref, sum_ref)
 
     def one(target, carry):
         total = one_target(target)
@@ -376,7 +401,7 @@
     list_ref, state_ref, state_list_ref, spread_ref, sum_ref, fold_ref, *, share,
 ):
     cells, _, slots = own_ref.shape
-    counts = [count_ref[p] for p in np.ndindex(count_ref.shape)]
+    counts = [count_ref[c] for c in range(cells)]
     for cell in range(cells):
         density = rho_ref[*own_place(cell, rho_ref.shape[:3])]
         state_ref[cell] = state_tile(density, own_ref[cell, pl.ds(7, 1), :])
@@ -384,16 +409,16 @@
         list(enumerate(counts)), [own_ref, state_ref], [list_ref, state_list_ref], [0.0, 1.0], 1
     )
 
-    def one_spread(chunk, carry):
+    rows = rows_of(chunks, share)
+
+    def one_spread(chunk):
         spread_chunk(list_ref[chunk], range(7), spread_ref, chunk)
         spread_chunk(state_list_ref[chunk], range(3), spread_ref, chunk, 7)
-        return carry
-
-    rows = rows_of(chunks, share)
-    lax.fori_loop(*rows, one_spread, 0)
+
+    in_twos(rows, one_spread)
 
     def pair(row, chunk, both):
-        mine = [spread_ref[n, row] for n in (0, 1, 2, 3, 4, 5, 7, 8, 9)]
+        mine = [spread_ref[n, rows_at(row), :] for n in (0, 1, 2, 3, 4, 5, 7, 8, 9)]
         far = [list_ref[chunk, pl.ds(n, 1), :] for n in range(6)]
         far += [state_list_ref[chunk, pl.ds(n, 1), :] for n in range(3)]
         factor, apart = pair_force(mine, far)
@@ -401,7 +426,7 @@
         by_row = [weight * a for a in apart]
         if not both:
             return by_row, None
-        weight = spread_ref[6, row] * factor
+        weight = spread_ref[6, rows_at(row), :] * factor
         return by_row, [-(weight * a) for a in apart]
 
     pairs_within(chunks, rows, 3, pair, sum_ref, fold_ref)
@@ -433,7 +458,7 @@
         density = density_ref[*own_place(target, sizes)]
         spread(state_tile(density, own_ref[target, pl.ds(7, 1), :]), range(3), spread_ref, 6)
         return force_of(
-            count_ref[*cell_place(target, sizes)], steps, lists_ref.at[target], state_list_ref, spread_ref, sum_ref
+            count_ref[target], steps, lists_ref.at[target], state_list_ref, spread_ref, sum_ref
         )
 
     def one(target, carry):
@@ -458,11 +483,14 @@
     cells = sizes[0] * sizes[1] * sizes[2]
     wide = (sizes[0] + 2) * (sizes[1] + 2) * (sizes[2] + 2)
     assert all(size <= 2 for size in sizes)
-    packed = pl.pallas_call(
+    packed, own_counts = pl.pallas_call(
         pack_kernel,
-        out_shape=jax.ShapeDtypeStruct(sizes + (8, slots), jnp.float32),
+        out_shape=(
+            jax.ShapeDtypeStruct(sizes + (8, slots), jnp.float32),
+            jax.ShapeDtypeStruct((cells,), jnp.int32),
+        ),
         in_specs=[pl.BlockSpec(memory_space=pltpu.HBM)] * 5,
-        out_specs=VMEM,
+        out_specs=(VMEM, SMEM),
         scratch_shapes=[
             pltpu.SMEM(counts.shape, jnp.int32),
             pltpu.VMEM(positions.shape, jnp.float32),
@@ -473,7 +501,12 @@
         ],
         compiler_params=PARAMS,
         name="pack",
-    )(counts, positions, velocities, masses, entropy)
+    )(
+        *(
+            pltpu.with_memory_space_constraint(item, pltpu.HBM)
+            for item in (counts, positions, velocities, masses, entropy)
+        )
+    )
     own = packed.reshape(cells, 8, slots)
     table = jnp.asarray(halo_table(sizes))
     near = table.shape[1]
@@ -483,12 +516,14 @@
     def own_rows(fields):
         return pltpu.VMEM((fields, own_chunks, LANES, LANES), jnp.float32)
 
+    def own_spread(fields):
+        return pltpu.VMEM((fields, own_chunks * LANES + PAD, LANES), jnp.float32)
+
     def own_folds(outputs):
         return pltpu.VMEM((outputs, own_chunks, 8, LANES), jnp.float32)
 
-    halo_order = (("gz", 2), ("gx", 0), ("gy", 1))
-    spread3 = pltpu.VMEM((3, slots, LANES), jnp.float32)
-    spread9 = pltpu.VMEM((9, slots, LANES), jnp.float32)
+    spread3 = pltpu.VMEM((3, slots + PAD, LANES), jnp.float32)
+    spread9 = pltpu.VMEM((9, slots + PAD, LANES), jnp.float32)
     sums = pltpu.VMEM((slots, LANES), jnp.float32)
     three_sums = pltpu.VMEM((3, slots, LANES), jnp.float32)
     own_list = list_scratch(cells, slots)
@@ -499,13 +534,13 @@
         out_shape=jax.ShapeDtypeStruct((cells, slots), jnp.float32),
         in_specs=[SMEM, VMEM],
         out_specs=VMEM,
-        scratch_shapes=[own_list, own_rows(4), own_rows(1), own_folds(1)],
+        scratch_shapes=[own_list, own_spread(4), own_rows(1), own_folds(1)],
         compiler_params=PARAMS,
         cost_estimate=cost(pairs * cells, 22),
-    )(counts, own) for share in SHARES]
-    pieces = with_halo(packed, halo_order)
+    )(own_counts, own) for share in DENSITY_SHARES]
+    pieces = with_halo(packed, ORDER)
     result, density, grid, grid_counts, lists = pl.pallas_call(
-        functools.partial(density_halo, sizes=sizes, parts=len(SHARES)),
+        functools.partial(density_halo, sizes=sizes, parts=len(DENSITY_SHARES)),
         out_shape=(
             jax.ShapeDtypeStruct(masses.shape, jnp.float32),
             jax.ShapeDtypeStruct(masses.shape, jnp.float32),
@@ -513,13 +548,13 @@
             jax.ShapeDtypeStruct((wide,), jnp.int32),
             jax.ShapeDtypeStruct((cells,) + halo_list.shape, jnp.float32),
         ),
-        in_specs=[SMEM, SMEM] + [VMEM] * (4 + len(SHARES)),
+        in_specs=[SMEM, SMEM] + [VMEM] * (4 + len(DENSITY_SHARES)),
         out_specs=(VMEM, VMEM, VMEM, SMEM, VMEM),
         scratch_shapes=[spread3, sums],
         compiler_params=PARAMS,
         cost_estimate=cost(pairs * near, 22),
         name="density_halo",
-    )(counts, table, own, *partials, *pieces)
+    )(own_counts, table, own, *partials, *pieces)
     partials = [pl.pallas_call(
         functools.partial(force_own, share=share),
         out_shape=jax.ShapeDtypeStruct((3, cells, slots), jnp.float32),
@@ -527,16 +562,16 @@
         out_specs=VMEM,
         scratch_shapes=[
             own_list, pltpu.VMEM((cells, 8, slots), jnp.float32), own_list,
-            own_rows(10), own_rows(3), own_folds(3),
+            own_spread(10), own_rows(3), own_folds(3),
         ],
         compiler_params=PARAMS,
         cost_estimate=cost(pairs * cells, 50),
-    )(counts, own, density) for share in SHARES]
-    pieces = with_halo(density, halo_order)
+    )(own_counts, own, density) for share in FORCE_SHARES]
+    pieces = with_halo(density, ORDER)
     acceleration = pl.pallas_call(
-        functools.partial(force_halo, sizes=sizes, parts=len(SHARES)),
+        functools.partial(force_halo, sizes=sizes, parts=len(FORCE_SHARES)),
         out_shape=jax.ShapeDtypeStruct(positions.shape, jnp.float32),
-        in_specs=[SMEM, SMEM, VMEM, VMEM, SMEM] + [VMEM] * (5 + len(SHARES)),
+        in_specs=[SMEM, SMEM, VMEM, VMEM, SMEM] + [VMEM] * (5 + len(FORCE_SHARES)),
         out_specs=VMEM,
         scratch_shapes=[
             pltpu.VMEM((wide, 8, slots), jnp.float32), halo_list,
@@ -545,7 +580,7 @@
         compiler_params=PARAMS,
         cost_estimate=cost(pairs * near, 50),
         name="force_halo",
-    )(counts, table, own, density, grid_counts, grid, lists, *partials, *pieces)
+    )(own_counts, table, own, density, grid_counts, grid, lists, *partials, *pieces)
     return (result, acceleration)
 
 

time: 107 us -> 101 us (0.944)
  waiting for transfers between devices: 5.7 us -> 9.74 us
  starting transfers between devices: 9.98 us -> 6.01 us
  local copies, waits for them, and re-layouts: 3.6 us -> 0.09 us
  Pallas kernels: 86 us -> 84.2 us
    ppermute x4, starting transfers between devices: 7.18 us -> 2.73 us  [with_halo(): high = lax.ppermute(first, axis, shifted(count, -1))]
    unnamed x12 -> x6, local copies, waits for them, and re-layouts: 3.55 us -> 0.02 us
    ppermute x4, waiting for transfers between devices: 0.01 us -> 3.3 us  [with_halo(): high = lax.ppermute(first, axis, shifted(count, -1))]
    pallas_call x3, Pallas kernels: 12.8 us -> 11.5 us  [per_device(): pl.pallas_call(functools.partial(density_own, share=share), out_shape=jax...]
  transfers between devices with their start and end apart: 10 -> 10, of which waited for: 2 -> 3; matrix products, arithmetic and copies ran while one was open for 0% -> 0% of each run, Pallas kernels for 34% -> 34%
where the time goes in v2:
time: 101 us
  Pallas kernels  84.2 us (83%)
  waiting for transfers between devices  9.74 us (10%)
  starting transfers between devices  6.01 us (6%)
    pallas_call x1, Pallas kernels, per_device(): pl.pallas_call(functools.partial(force_halo, sizes=sizes, parts=len(FORCE...  32.4 us
    pallas_call x3, Pallas kernels, per_device(): pl.pallas_call(functools.partial(force_own, share=share), out_shape=jax.S...  22.5 us
    pallas_call x1, Pallas kernels, per_device(): pl.pallas_call(functools.partial(density_halo, sizes=sizes, parts=len(DEN...  16.4 us
    pallas_call x3, Pallas kernels, per_device(): pl.pallas_call(functools.partial(density_own, share=share), out_shape=jax...  11.5 us
    ppermute x2, waiting for transfers between devices, with_halo(): other = lax.ppermute(block, axis, shifted(2, 1))  4.44 us
    ppermute x4, waiting for transfers between devices, with_halo(): high = lax.ppermute(first, axis, shifted(count, -1))  3.3 us
    ppermute x4, starting transfers between devices, with_halo(): high = lax.ppermute(first, axis, shifted(count, -1))  2.73 us
    ppermute x4, starting transfers between devices, with_halo(): low = lax.ppermute(last, axis, shifted(count, 1))  2.68 us
  transfers between devices with their start and end apart: 10, of which 3 were waited for; matrix products, arithmetic and copies ran while one was open for 0% of the time, Pallas kernels for 34%

profile of v2, /device:TPU:6, one launch (start us, length us, event | category | flops | bytes accessed | tf_op | source)
XLA Modules:
  0.0 101.0 jit_solution(5143995578280921054)
XLA Ops:
  0.6 1.4 %pack.1 = (f32[2,2,2,8,256]{4,3,2,1,0:T(8,128)S(1)}, s32[8]{0:T(128)S(1)}) custom-call(s32[2,2,2]{2,1,0:T(2,128)} %count_hbm.1, f32[3,2,2,2,256]{4,3,2,1,0:T(2,128)} %position_hbm.1, f32[3,2,2,2,256]{4,3,2,1,0:T(2,128)} %velocity_hbm.1, f32[2,2,2,256]{3,2,1,0:T(2,128)} %mass_hbm.1, f32[2,2,2,256]{3,2,1,0:T(2,128)} %entropy_hbm.1), custom_call_target="tpu_custom_call" | custom-call | tf_op jit(solution)/shard_map/pack/pallas_call | solution.py:486
  2.1 1.6 %collective-permute-start = (f32[2,1,2,8,256]{4,3,2,1,0:T(8,128)S(1)}, f32[2,1,2,8,256]{4,3,2,1,0:T(8,128)S(1)}, u32[]{:S(2)}, u32[]{:S(2)}) collective-permute-start(f32[2,1,2,8,256]{4,3,2,1,0:T(8,128)S(1)} %get-tuple-element.21), channel_id=1, source_target_pairs={{0,2},{2,4},{4,6},{6,0},{1,3},{3,5},{5,7},{7,1},{8,10},{10,12},{12... | collective-permute-start | bytes 98312 | tf_op jit(solution)/shard_map/ppermute | solution.py:47
  3.7 2.2 %collective-permute-start.1 = (f32[2,1,2,8,256]{4,3,2,1,0:T(8,128)S(1)}, f32[2,1,2,8,256]{4,3,2,1,0:T(8,128)S(1)}, u32[]{:S(2)}, u32[]{:S(2)}) collective-permute-start(f32[2,1,2,8,256]{4,3,2,1,0:T(8,128)S(1)} %get-tuple-element.20), channel_id=1, source_target_pairs={{0,6},{2,0},{4,2},{6,4},{1,7},{3,1},{5,3},{7,5},{8,14},{10,8},{12,... | collective-permute-start | bytes 98312 | tf_op jit(solution)/shard_map/ppermute | solution.py:48
  6.0 2.0 %collective-permute-done = f32[2,1,2,8,256]{4,3,2,1,0:T(8,128)S(1)} collective-permute-done((f32[2,1,2,8,256]{4,3,2,1,0:T(8,128)S(1)}, f32[2,1,2,8,256]{4,3,2,1,0:T(8,128)S(1)}, u32[]{:S(2)}, u32[]{:S(2)}) %collective-permute-start) | collective-permute-done | bytes 32800 | tf_op jit(solution)/shard_map/ppermute | solution.py:47
  8.0 0.0 collective-permute-done.1
  8.0 0.6 collective-permute-start.2
  8.6 4.4 %collective-permute-done.2 = f32[2,4,2,8,256]{4,3,2,1,0:T(8,128)S(1)} collective-permute-done((f32[2,4,2,8,256]{4,3,2,1,0:T(8,128)S(1)}, f32[2,4,2,8,256]{4,3,2,1,0:T(8,128)S(1)}, u32[]{:S(2)}, u32[]{:S(2)}) %collective-permute-start.2) | collective-permute-done | bytes 131104 | tf_op jit(solution)/shard_map/ppermute | solution.py:41
  13.1 0.1 collective-permute-start.4
  13.2 0.5 collective-permute-start.3
  13.7 4.9 %shard_map.79.refs_2_ = f32[8,256]{1,0:T(8,128)S(1)} custom-call(s32[8]{0:T(128)S(1)} %get-tuple-element.9.count_ref, f32[8,8,256]{2,1,0:T(8,128)S(1)} %bitcast.1), custom_call_target="tpu_custom_call" | custom-call | flops 92274688 | bytes 1048576 | tf_op jit(solution)/shard_map/pallas_call | solution.py:532
  18.5 2.5 %shard_map.78.refs_1_ = f32[8,256]{1,0:T(8,128)S(1)} custom-call(s32[8]{0:T(128)S(1)} %get-tuple-element.9.count_ref, f32[8,8,256]{2,1,0:T(8,128)S(1)} %bitcast.2), custom_call_target="tpu_custom_call" | custom-call | flops 92274688 | bytes 1048576 | tf_op jit(solution)/shard_map/pallas_call | solution.py:532
  21.0 0.0 copy-start
  21.0 4.2 %shard_map.77.refs_0_ = f32[8,256]{1,0:T(8,128)S(1)} custom-call(s32[8]{0:T(128)S(1)} %get-tuple-element.9.count_ref, f32[8,8,256]{2,1,0:T(8,128)S(1)} %bitcast.3), custom_call_target="tpu_custom_call" | custom-call | flops 92274688 | bytes 1048576 | tf_op jit(solution)/shard_map/pallas_call | solution.py:532
  25.2 0.0 collective-permute-done.4.refs_5_
  25.2 0.0 collective-permute-done.3.refs_4_
  25.2 0.0 copy-done
  25.2 16.4 %density_halo.1 = (f32[2,2,2,256]{3,2,1,0:T(2,128)}, f32[2,2,2,256]{3,2,1,0:T(2,128)S(1)}, f32[64,8,256]{2,1,0:T(8,128)S(1)}, s32[64]{0:T(128)S(1)}, f32[8,42,8,128]{3,2,1,0:T(8,128)S(1)}) custom-call(s32[8]{0:T(128)S(1)} %get-tuple-element.9.count_ref, s32[8,19]{1,0:T(8,128)S(1)} %copy-done, f32[8,8,256]{2,1,0:T(8,128)S(1)} %bitcast.4, ...), custom_call_target="tpu_custom_call" | custom-call | flops 219152384 | bytes 1048576 | tf_op jit(solution)/shard_map/density_halo/pallas_call | solution.py:542
  41.6 0.1 collective-permute-start.5
  41.7 11.9 %shard_map.82.refs_2_ = f32[3,8,256]{2,1,0:T(8,128)S(1)} custom-call(s32[8]{0:T(128)S(1)} %get-tuple-element.9.count_ref, f32[8,8,256]{2,1,0:T(8,128)S(1)} %bitcast.5, f32[2,2,2,256]{3,2,1,0:T(2,128)S(1)} %get-tuple-element.12.rho_ref.density_ref), custom_call_target="tpu_custom_call" | custom-call | flops 209715200 | bytes 1048576 | tf_op jit(solution)/shard_map/pallas_call | solution.py:558
  53.6 0.4 collective-permute-start.6
  54.0 0.0 collective-permute-done.5
  54.0 3.3 %collective-permute-done.6 = f32[2,1,2,256]{3,2,1,0:T(2,128)S(1)} collective-permute-done((f32[2,1,2,256]{3,2,1,0:T(2,128)S(1)}, f32[2,1,2,256]{3,2,1,0:T(2,128)S(1)}, u32[]{:S(2)}, u32[]{:S(2)}) %collective-permute-start.6) | collective-permute-done | bytes 4128 | tf_op jit(solution)/shard_map/ppermute | solution.py:48
  57.3 0.0 collective-permute-start.7
  57.3 5.0 %shard_map.81.refs_1_ = f32[3,8,256]{2,1,0:T(8,128)S(1)} custom-call(s32[8]{0:T(128)S(1)} %get-tuple-element.9.count_ref, f32[8,8,256]{2,1,0:T(8,128)S(1)} %bitcast.6, f32[2,2,2,256]{3,2,1,0:T(2,128)S(1)} %get-tuple-element.12.rho_ref.density_ref), custom_call_target="tpu_custom_call" | custom-call | flops 209715200 | bytes 1048576 | tf_op jit(solution)/shard_map/pallas_call | solution.py:558
  62.3 0.0 collective-permute-done.7
  62.4 0.1 collective-permute-start.9
  62.4 0.5 collective-permute-start.8
  62.9 5.6 %shard_map.80.refs_0_ = f32[3,8,256]{2,1,0:T(8,128)S(1)} custom-call(s32[8]{0:T(128)S(1)} %get-tuple-element.9.count_ref, f32[8,8,256]{2,1,0:T(8,128)S(1)} %bitcast.7, f32[2,2,2,256]{3,2,1,0:T(2,128)S(1)} %get-tuple-element.12.rho_ref.density_ref), custom_call_target="tpu_custom_call" | custom-call | flops 209715200 | bytes 1048576 | tf_op jit(solution)/shard_map/pallas_call | solution.py:558
  68.6 0.0 collective-permute-done.9.refs_5_
  68.6 0.0 collective-permute-done.8.refs_4_
  68.6 32.4 %force_halo.1 = f32[3,2,2,2,256]{4,3,2,1,0:T(2,128)} custom-call(s32[8]{0:T(128)S(1)} %get-tuple-element.9.count_ref, s32[8,19]{1,0:T(8,128)S(1)} %copy-done, f32[8,8,256]{2,1,0:T(8,128)S(1)} %bitcast.8, f32[2,2,2,256]{3,2,1,0:T(2,128)S(1)} %get-tuple-element.12.rho_ref.density_ref, s32[64]{0:T(128)S(1)} %get-tuple-element.13.grid_count_ref, ...), custom_call_target="tpu_custom_call" | custom-call | flops 498073600 | bytes 1048576 | tf_op jit(solution)/shard_map/force_halo/pallas_call | solution.py:571
  (14 shorter events, 0.1 us)
Async XLA Ops:
  2.1 5.9 %collective-permute-start = (f32[2,1,2,8,256]{4,3,2,1,0:T(8,128)S(1)}, f32[2,1,2,8,256]{4,3,2,1,0:T(8,128)S(1)}, u32[]{:S(2)}, u32[]{:S(2)}) collective-permute-start(f32[2,1,2,8,256]{4,3,2,1,0:T(8,128)S(1)} %get-tuple-element.21), channel_id=1, source_target_pairs={{0,2},{2,4},{4,6},{6,0},{1,3},{3,5},{5,7},{7,1},{8,10},{10,12},{12... | collective-permute-start | bytes 98312 | tf_op jit(solution)/shard_map/ppermute | solution.py:47
  3.7 4.3 %collective-permute-start.1 = (f32[2,1,2,8,256]{4,3,2,1,0:T(8,128)S(1)}, f32[2,1,2,8,256]{4,3,2,1,0:T(8,128)S(1)}, u32[]{:S(2)}, u32[]{:S(2)}) collective-permute-start(f32[2,1,2,8,256]{4,3,2,1,0:T(8,128)S(1)} %get-tuple-element.20), channel_id=1, source_target_pairs={{0,6},{2,0},{4,2},{6,4},{1,7},{3,1},{5,3},{7,5},{8,14},{10,8},{12,... | collective-permute-start | bytes 98312 | tf_op jit(solution)/shard_map/ppermute | solution.py:48
  8.0 5.0 %collective-permute-start.2 = (f32[2,4,2,8,256]{4,3,2,1,0:T(8,128)S(1)}, f32[2,4,2,8,256]{4,3,2,1,0:T(8,128)S(1)}, u32[]{:S(2)}, u32[]{:S(2)}) collective-permute-start(f32[2,4,2,8,256]{4,3,2,1,0:T(8,128)S(1)} %constant_dynamic-update-slice_fusion), channel_id=1, source_target_pairs={{0,1},{1,0},{2,3},{3,2},{4,5},{5,4},{6,7},{7,6},{8,9},{9,8},{10,11... | collective-permute-start | bytes 393224 | tf_op jit(solution)/shard_map/ppermute | solution.py:41
  13.1 12.1 %collective-permute-start.4 = (f32[1,4,4,8,256]{4,3,2,1,0:T(8,128)S(1)}, f32[1,4,4,8,256]{4,3,2,1,0:T(8,128)S(1)}, u32[]{:S(2)}, u32[]{:S(2)}) collective-permute-start(f32[1,4,4,8,256]{4,3,2,1,0:T(8,128)S(1)} %get-tuple-element.16), channel_id=1, source_target_pairs={{0,24},{8,0},{16,8},{24,16},{1,25},{9,1},{17,9},{25,17},{2,26},{10... | collective-permute-start | bytes 393224 | tf_op jit(solution)/shard_map/ppermute | solution.py:48
  13.2 12.1 %collective-permute-start.3 = (f32[1,4,4,8,256]{4,3,2,1,0:T(8,128)S(1)}, f32[1,4,4,8,256]{4,3,2,1,0:T(8,128)S(1)}, u32[]{:S(2)}, u32[]{:S(2)}) collective-permute-start(f32[1,4,4,8,256]{4,3,2,1,0:T(8,128)S(1)} %get-tuple-element.17), channel_id=1, source_target_pairs={{0,8},{8,16},{16,24},{24,0},{1,9},{9,17},{17,25},{25,1},{2,10},{10... | collective-permute-start | bytes 393224 | tf_op jit(solution)/shard_map/ppermute | solution.py:47
  21.0 4.2 %copy-start = (s32[8,19]{1,0:T(8,128)S(1)}, s32[8,19]{1,0:T(8,128)}, u32[]{:S(2)}) copy-start(s32[8,19]{1,0:T(8,128)} %constant.2.clone.table_ref) | copy-start | bytes 1828
  41.6 12.3 %collective-permute-start.5 = (f32[2,1,2,256]{3,2,1,0:T(2,128)S(1)}, f32[2,1,2,256]{3,2,1,0:T(2,128)S(1)}, u32[]{:S(2)}, u32[]{:S(2)}) collective-permute-start(f32[2,1,2,256]{3,2,1,0:T(2,128)S(1)} %get-tuple-element.27), channel_id=1, source_target_pairs={{0,2},{2,4},{4,6},{6,0},{1,3},{3,5},{5,7},{7,1},{8,10},{10,12},{12... | collective-permute-start | bytes 12296 | tf_op jit(solution)/shard_map/ppermute | solution.py:47
  53.6 3.7 %collective-permute-start.6 = (f32[2,1,2,256]{3,2,1,0:T(2,128)S(1)}, f32[2,1,2,256]{3,2,1,0:T(2,128)S(1)}, u32[]{:S(2)}, u32[]{:S(2)}) collective-permute-start(f32[2,1,2,256]{3,2,1,0:T(2,128)S(1)} %get-tuple-element.26), channel_id=1, source_target_pairs={{0,6},{2,0},{4,2},{6,4},{1,7},{3,1},{5,3},{7,5},{8,14},{10,8},{12,... | collective-permute-start | bytes 12296 | tf_op jit(solution)/shard_map/ppermute | solution.py:48
  57.3 5.0 %collective-permute-start.7 = (f32[2,4,2,256]{3,2,1,0:T(2,128)S(1)}, f32[2,4,2,256]{3,2,1,0:T(2,128)S(1)}, u32[]{:S(2)}, u32[]{:S(2)}) collective-permute-start(f32[2,4,2,256]{3,2,1,0:T(2,128)S(1)} %constant_dynamic-update-slice_fusion.3), channel_id=1, source_target_pairs={{0,1},{1,0},{2,3},{3,2},{4,5},{5,4},{6,7},{7,6},{8,9},{9,8},{10,11... | collective-permute-start | bytes 49160 | tf_op jit(solution)/shard_map/ppermute | solution.py:41
  62.4 6.2 %collective-permute-start.9 = (f32[1,4,4,256]{3,2,1,0:T(4,128)S(1)}, f32[1,4,4,256]{3,2,1,0:T(4,128)S(1)}, u32[]{:S(2)}, u32[]{:S(2)}) collective-permute-start(f32[1,4,4,256]{3,2,1,0:T(4,128)S(1)} %get-tuple-element.22), channel_id=1, source_target_pairs={{0,24},{8,0},{16,8},{24,16},{1,25},{9,1},{17,9},{25,17},{2,26},{10... | collective-permute-start | bytes 49160 | tf_op jit(solution)/shard_map/ppermute | solution.py:48
  62.4 6.2 %collective-permute-start.8 = (f32[1,4,4,256]{3,2,1,0:T(4,128)S(1)}, f32[1,4,4,256]{3,2,1,0:T(4,128)S(1)}, u32[]{:S(2)}, u32[]{:S(2)}) collective-permute-start(f32[1,4,4,256]{3,2,1,0:T(4,128)S(1)} %get-tuple-element.23), channel_id=1, source_target_pairs={{0,8},{8,16},{16,24},{24,0},{1,9},{9,17},{17,25},{25,1},{2,10},{10... | collective-permute-start | bytes 49160 | tf_op jit(solution)/shard_map/ppermute | solution.py:47

commit v3 on v2

--- a/solution.py
+++ b/solution.py
@@ -27,6 +27,7 @@
 VMEM = pl.BlockSpec(memory_space=pltpu.VMEM)
 SMEM = pl.BlockSpec(memory_space=pltpu.SMEM)
 PARAMS = pltpu.CompilerParams(vmem_limit_bytes=24 << 20)
+DENSITY_PARAMS = pltpu.CompilerParams(vmem_limit_bytes=24 << 20)
 
 
 def shifted(size, step):
@@ -535,7 +536,7 @@
         in_specs=[SMEM, VMEM],
         out_specs=VMEM,
         scratch_shapes=[own_list, own_spread(4), own_rows(1), own_folds(1)],
-        compiler_params=PARAMS,
+        compiler_params=DENSITY_PARAMS,
         cost_estimate=cost(pairs * cells, 22),
     )(own_counts, own) for share in DENSITY_SHARES]
     pieces = with_halo(packed, ORDER)
@@ -551,7 +552,7 @@
         in_specs=[SMEM, SMEM] + [VMEM] * (4 + len(DENSITY_SHARES)),
         out_specs=(VMEM, VMEM, VMEM, SMEM, VMEM),
         scratch_shapes=[spread3, sums],
-        compiler_params=PARAMS,
+        compiler_params=DENSITY_PARAMS,
         cost_estimate=cost(pairs * near, 22),
         name="density_halo",
     )(own_counts, table, own, *partials, *pieces)

time: 101 us -> 101 us (level)
  no operation moved by 1% of the time
where the time goes in v3:
time: 101 us
  Pallas kernels  84.2 us (83%)
  waiting for transfers between devices  9.74 us (10%)
  starting transfers between devices  6.01 us (6%)
    pallas_call x1, Pallas kernels, per_device(): pl.pallas_call(functools.partial(force_halo, sizes=sizes, parts=len(FORCE...  32.4 us
    pallas_call x3, Pallas kernels, per_device(): pl.pallas_call(functools.partial(force_own, share=share), out_shape=jax.S...  22.5 us
    pallas_call x1, Pallas kernels, per_device(): pl.pallas_call(functools.partial(density_halo, sizes=sizes, parts=len(DEN...  16.4 us
    pallas_call x3, Pallas kernels, per_device(): pl.pallas_call(functools.partial(density_own, share=share), out_shape=jax...  11.5 us
    ppermute x2, waiting for transfers between devices, with_halo(): other = lax.ppermute(block, axis, shifted(2, 1))  4.44 us
    ppermute x4, waiting for transfers between devices, with_halo(): high = lax.ppermute(first, axis, shifted(count, -1))  3.3 us
    ppermute x4, starting transfers between devices, with_halo(): high = lax.ppermute(first, axis, shifted(count, -1))  2.73 us
    ppermute x4, starting transfers between devices, with_halo(): low = lax.ppermute(last, axis, shifted(count, 1))  2.68 us
  transfers between devices with their start and end apart: 10, of which 3 were waited for; matrix products, arithmetic and copies ran while one was open for 0% of the time, Pallas kernels for 34%

profile of v3, /device:TPU:6, one launch (start us, length us, event | category | flops | bytes accessed | tf_op | source)
XLA Modules:
  0.0 101.0 jit_solution(5143995578280921054)
XLA Ops:
  0.6 1.4 %pack.1 = (f32[2,2,2,8,256]{4,3,2,1,0:T(8,128)S(1)}, s32[8]{0:T(128)S(1)}) custom-call(s32[2,2,2]{2,1,0:T(2,128)} %count_hbm.1, f32[3,2,2,2,256]{4,3,2,1,0:T(2,128)} %position_hbm.1, f32[3,2,2,2,256]{4,3,2,1,0:T(2,128)} %velocity_hbm.1, f32[2,2,2,256]{3,2,1,0:T(2,128)} %mass_hbm.1, f32[2,2,2,256]{3,2,1,0:T(2,128)} %entropy_hbm.1), custom_call_target="tpu_custom_call" | custom-call | tf_op jit(solution)/shard_map/pack/pallas_call | solution.py:487
  2.1 1.6 %collective-permute-start = (f32[2,1,2,8,256]{4,3,2,1,0:T(8,128)S(1)}, f32[2,1,2,8,256]{4,3,2,1,0:T(8,128)S(1)}, u32[]{:S(2)}, u32[]{:S(2)}) collective-permute-start(f32[2,1,2,8,256]{4,3,2,1,0:T(8,128)S(1)} %get-tuple-element.21), channel_id=1, source_target_pairs={{0,2},{2,4},{4,6},{6,0},{1,3},{3,5},{5,7},{7,1},{8,10},{10,12},{12... | collective-permute-start | bytes 98312 | tf_op jit(solution)/shard_map/ppermute | solution.py:48
  3.7 2.2 %collective-permute-start.1 = (f32[2,1,2,8,256]{4,3,2,1,0:T(8,128)S(1)}, f32[2,1,2,8,256]{4,3,2,1,0:T(8,128)S(1)}, u32[]{:S(2)}, u32[]{:S(2)}) collective-permute-start(f32[2,1,2,8,256]{4,3,2,1,0:T(8,128)S(1)} %get-tuple-element.20), channel_id=1, source_target_pairs={{0,6},{2,0},{4,2},{6,4},{1,7},{3,1},{5,3},{7,5},{8,14},{10,8},{12,... | collective-permute-start | bytes 98312 | tf_op jit(solution)/shard_map/ppermute | solution.py:49
  6.0 2.0 %collective-permute-done = f32[2,1,2,8,256]{4,3,2,1,0:T(8,128)S(1)} collective-permute-done((f32[2,1,2,8,256]{4,3,2,1,0:T(8,128)S(1)}, f32[2,1,2,8,256]{4,3,2,1,0:T(8,128)S(1)}, u32[]{:S(2)}, u32[]{:S(2)}) %collective-permute-start) | collective-permute-done | bytes 32800 | tf_op jit(solution)/shard_map/ppermute | solution.py:48
  8.0 0.0 collective-permute-done.1
  8.0 0.6 collective-permute-start.2
  8.6 4.4 %collective-permute-done.2 = f32[2,4,2,8,256]{4,3,2,1,0:T(8,128)S(1)} collective-permute-done((f32[2,4,2,8,256]{4,3,2,1,0:T(8,128)S(1)}, f32[2,4,2,8,256]{4,3,2,1,0:T(8,128)S(1)}, u32[]{:S(2)}, u32[]{:S(2)}) %collective-permute-start.2) | collective-permute-done | bytes 131104 | tf_op jit(solution)/shard_map/ppermute | solution.py:42
  13.1 0.1 collective-permute-start.4
  13.2 0.5 collective-permute-start.3
  13.7 4.9 %shard_map.79.refs_2_ = f32[8,256]{1,0:T(8,128)S(1)} custom-call(s32[8]{0:T(128)S(1)} %get-tuple-element.9.count_ref, f32[8,8,256]{2,1,0:T(8,128)S(1)} %bitcast.1), custom_call_target="tpu_custom_call" | custom-call | flops 92274688 | bytes 1048576 | tf_op jit(solution)/shard_map/pallas_call | solution.py:533
  18.5 2.5 %shard_map.78.refs_1_ = f32[8,256]{1,0:T(8,128)S(1)} custom-call(s32[8]{0:T(128)S(1)} %get-tuple-element.9.count_ref, f32[8,8,256]{2,1,0:T(8,128)S(1)} %bitcast.2), custom_call_target="tpu_custom_call" | custom-call | flops 92274688 | bytes 1048576 | tf_op jit(solution)/shard_map/pallas_call | solution.py:533
  21.0 0.0 copy-start
  21.0 4.2 %shard_map.77.refs_0_ = f32[8,256]{1,0:T(8,128)S(1)} custom-call(s32[8]{0:T(128)S(1)} %get-tuple-element.9.count_ref, f32[8,8,256]{2,1,0:T(8,128)S(1)} %bitcast.3), custom_call_target="tpu_custom_call" | custom-call | flops 92274688 | bytes 1048576 | tf_op jit(solution)/shard_map/pallas_call | solution.py:533
  25.2 0.0 collective-permute-done.4.refs_5_
  25.2 0.0 collective-permute-done.3.refs_4_
  25.2 0.0 copy-done
  25.2 16.4 %density_halo.1 = (f32[2,2,2,256]{3,2,1,0:T(2,128)}, f32[2,2,2,256]{3,2,1,0:T(2,128)S(1)}, f32[64,8,256]{2,1,0:T(8,128)S(1)}, s32[64]{0:T(128)S(1)}, f32[8,42,8,128]{3,2,1,0:T(8,128)S(1)}) custom-call(s32[8]{0:T(128)S(1)} %get-tuple-element.9.count_ref, s32[8,19]{1,0:T(8,128)S(1)} %copy-done, f32[8,8,256]{2,1,0:T(8,128)S(1)} %bitcast.4, ...), custom_call_target="tpu_custom_call" | custom-call | flops 219152384 | bytes 1048576 | tf_op jit(solution)/shard_map/density_halo/pallas_call | solution.py:543
  41.6 0.1 collective-permute-start.5
  41.7 11.9 %shard_map.82.refs_2_ = f32[3,8,256]{2,1,0:T(8,128)S(1)} custom-call(s32[8]{0:T(128)S(1)} %get-tuple-element.9.count_ref, f32[8,8,256]{2,1,0:T(8,128)S(1)} %bitcast.5, f32[2,2,2,256]{3,2,1,0:T(2,128)S(1)} %get-tuple-element.12.rho_ref.density_ref), custom_call_target="tpu_custom_call" | custom-call | flops 209715200 | bytes 1048576 | tf_op jit(solution)/shard_map/pallas_call | solution.py:559
  53.6 0.4 collective-permute-start.6
  54.0 0.0 collective-permute-done.5
  54.0 3.3 %collective-permute-done.6 = f32[2,1,2,256]{3,2,1,0:T(2,128)S(1)} collective-permute-done((f32[2,1,2,256]{3,2,1,0:T(2,128)S(1)}, f32[2,1,2,256]{3,2,1,0:T(2,128)S(1)}, u32[]{:S(2)}, u32[]{:S(2)}) %collective-permute-start.6) | collective-permute-done | bytes 4128 | tf_op jit(solution)/shard_map/ppermute | solution.py:49
  57.3 0.0 collective-permute-start.7
  57.3 5.0 %shard_map.81.refs_1_ = f32[3,8,256]{2,1,0:T(8,128)S(1)} custom-call(s32[8]{0:T(128)S(1)} %get-tuple-element.9.count_ref, f32[8,8,256]{2,1,0:T(8,128)S(1)} %bitcast.6, f32[2,2,2,256]{3,2,1,0:T(2,128)S(1)} %get-tuple-element.12.rho_ref.density_ref), custom_call_target="tpu_custom_call" | custom-call | flops 209715200 | bytes 1048576 | tf_op jit(solution)/shard_map/pallas_call | solution.py:559
  62.3 0.0 collective-permute-done.7
  62.4 0.1 collective-permute-start.9
  62.4 0.5 collective-permute-start.8
  62.9 5.6 %shard_map.80.refs_0_ = f32[3,8,256]{2,1,0:T(8,128)S(1)} custom-call(s32[8]{0:T(128)S(1)} %get-tuple-element.9.count_ref, f32[8,8,256]{2,1,0:T(8,128)S(1)} %bitcast.7, f32[2,2,2,256]{3,2,1,0:T(2,128)S(1)} %get-tuple-element.12.rho_ref.density_ref), custom_call_target="tpu_custom_call" | custom-call | flops 209715200 | bytes 1048576 | tf_op jit(solution)/shard_map/pallas_call | solution.py:559
  68.6 0.0 collective-permute-done.9.refs_5_
  68.6 0.0 collective-permute-done.8.refs_4_
  68.6 32.4 %force_halo.1 = f32[3,2,2,2,256]{4,3,2,1,0:T(2,128)} custom-call(s32[8]{0:T(128)S(1)} %get-tuple-element.9.count_ref, s32[8,19]{1,0:T(8,128)S(1)} %copy-done, f32[8,8,256]{2,1,0:T(8,128)S(1)} %bitcast.8, f32[2,2,2,256]{3,2,1,0:T(2,128)S(1)} %get-tuple-element.12.rho_ref.density_ref, s32[64]{0:T(128)S(1)} %get-tuple-element.13.grid_count_ref, ...), custom_call_target="tpu_custom_call" | custom-call | flops 498073600 | bytes 1048576 | tf_op jit(solution)/shard_map/force_halo/pallas_call | solution.py:572
  (14 shorter events, 0.1 us)
Async XLA Ops:
  2.1 5.9 %collective-permute-start = (f32[2,1,2,8,256]{4,3,2,1,0:T(8,128)S(1)}, f32[2,1,2,8,256]{4,3,2,1,0:T(8,128)S(1)}, u32[]{:S(2)}, u32[]{:S(2)}) collective-permute-start(f32[2,1,2,8,256]{4,3,2,1,0:T(8,128)S(1)} %get-tuple-element.21), channel_id=1, source_target_pairs={{0,2},{2,4},{4,6},{6,0},{1,3},{3,5},{5,7},{7,1},{8,10},{10,12},{12... | collective-permute-start | bytes 98312 | tf_op jit(solution)/shard_map/ppermute | solution.py:48
  3.7 4.3 %collective-permute-start.1 = (f32[2,1,2,8,256]{4,3,2,1,0:T(8,128)S(1)}, f32[2,1,2,8,256]{4,3,2,1,0:T(8,128)S(1)}, u32[]{:S(2)}, u32[]{:S(2)}) collective-permute-start(f32[2,1,2,8,256]{4,3,2,1,0:T(8,128)S(1)} %get-tuple-element.20), channel_id=1, source_target_pairs={{0,6},{2,0},{4,2},{6,4},{1,7},{3,1},{5,3},{7,5},{8,14},{10,8},{12,... | collective-permute-start | bytes 98312 | tf_op jit(solution)/shard_map/ppermute | solution.py:49
  8.0 5.0 %collective-permute-start.2 = (f32[2,4,2,8,256]{4,3,2,1,0:T(8,128)S(1)}, f32[2,4,2,8,256]{4,3,2,1,0:T(8,128)S(1)}, u32[]{:S(2)}, u32[]{:S(2)}) collective-permute-start(f32[2,4,2,8,256]{4,3,2,1,0:T(8,128)S(1)} %constant_dynamic-update-slice_fusion), channel_id=1, source_target_pairs={{0,1},{1,0},{2,3},{3,2},{4,5},{5,4},{6,7},{7,6},{8,9},{9,8},{10,11... | collective-permute-start | bytes 393224 | tf_op jit(solution)/shard_map/ppermute | solution.py:42
  13.1 12.1 %collective-permute-start.4 = (f32[1,4,4,8,256]{4,3,2,1,0:T(8,128)S(1)}, f32[1,4,4,8,256]{4,3,2,1,0:T(8,128)S(1)}, u32[]{:S(2)}, u32[]{:S(2)}) collective-permute-start(f32[1,4,4,8,256]{4,3,2,1,0:T(8,128)S(1)} %get-tuple-element.16), channel_id=1, source_target_pairs={{0,24},{8,0},{16,8},{24,16},{1,25},{9,1},{17,9},{25,17},{2,26},{10... | collective-permute-start | bytes 393224 | tf_op jit(solution)/shard_map/ppermute | solution.py:49
  13.2 12.1 %collective-permute-start.3 = (f32[1,4,4,8,256]{4,3,2,1,0:T(8,128)S(1)}, f32[1,4,4,8,256]{4,3,2,1,0:T(8,128)S(1)}, u32[]{:S(2)}, u32[]{:S(2)}) collective-permute-start(f32[1,4,4,8,256]{4,3,2,1,0:T(8,128)S(1)} %get-tuple-element.17), channel_id=1, source_target_pairs={{0,8},{8,16},{16,24},{24,0},{1,9},{9,17},{17,25},{25,1},{2,10},{10... | collective-permute-start | bytes 393224 | tf_op jit(solution)/shard_map/ppermute | solution.py:48
  21.0 4.2 %copy-start = (s32[8,19]{1,0:T(8,128)S(1)}, s32[8,19]{1,0:T(8,128)}, u32[]{:S(2)}) copy-start(s32[8,19]{1,0:T(8,128)} %constant.2.clone.table_ref) | copy-start | bytes 1828
  41.6 12.3 %collective-permute-start.5 = (f32[2,1,2,256]{3,2,1,0:T(2,128)S(1)}, f32[2,1,2,256]{3,2,1,0:T(2,128)S(1)}, u32[]{:S(2)}, u32[]{:S(2)}) collective-permute-start(f32[2,1,2,256]{3,2,1,0:T(2,128)S(1)} %get-tuple-element.27), channel_id=1, source_target_pairs={{0,2},{2,4},{4,6},{6,0},{1,3},{3,5},{5,7},{7,1},{8,10},{10,12},{12... | collective-permute-start | bytes 12296 | tf_op jit(solution)/shard_map/ppermute | solution.py:48
  53.6 3.7 %collective-permute-start.6 = (f32[2,1,2,256]{3,2,1,0:T(2,128)S(1)}, f32[2,1,2,256]{3,2,1,0:T(2,128)S(1)}, u32[]{:S(2)}, u32[]{:S(2)}) collective-permute-start(f32[2,1,2,256]{3,2,1,0:T(2,128)S(1)} %get-tuple-element.26), channel_id=1, source_target_pairs={{0,6},{2,0},{4,2},{6,4},{1,7},{3,1},{5,3},{7,5},{8,14},{10,8},{12,... | collective-permute-start | bytes 12296 | tf_op jit(solution)/shard_map/ppermute | solution.py:49
  57.3 5.0 %collective-permute-start.7 = (f32[2,4,2,256]{3,2,1,0:T(2,128)S(1)}, f32[2,4,2,256]{3,2,1,0:T(2,128)S(1)}, u32[]{:S(2)}, u32[]{:S(2)}) collective-permute-start(f32[2,4,2,256]{3,2,1,0:T(2,128)S(1)} %constant_dynamic-update-slice_fusion.3), channel_id=1, source_target_pairs={{0,1},{1,0},{2,3},{3,2},{4,5},{5,4},{6,7},{7,6},{8,9},{9,8},{10,11... | collective-permute-start | bytes 49160 | tf_op jit(solution)/shard_map/ppermute | solution.py:42
  62.4 6.2 %collective-permute-start.9 = (f32[1,4,4,256]{3,2,1,0:T(4,128)S(1)}, f32[1,4,4,256]{3,2,1,0:T(4,128)S(1)}, u32[]{:S(2)}, u32[]{:S(2)}) collective-permute-start(f32[1,4,4,256]{3,2,1,0:T(4,128)S(1)} %get-tuple-element.22), channel_id=1, source_target_pairs={{0,24},{8,0},{16,8},{24,16},{1,25},{9,1},{17,9},{25,17},{2,26},{10... | collective-permute-start | bytes 49160 | tf_op jit(solution)/shard_map/ppermute | solution.py:49
  62.4 6.2 %collective-permute-start.8 = (f32[1,4,4,256]{3,2,1,0:T(4,128)S(1)}, f32[1,4,4,256]{3,2,1,0:T(4,128)S(1)}, u32[]{:S(2)}, u32[]{:S(2)}) collective-permute-start(f32[1,4,4,256]{3,2,1,0:T(4,128)S(1)} %get-tuple-element.23), channel_id=1, source_target_pairs={{0,8},{8,16},{16,24},{24,0},{1,9},{9,17},{17,25},{25,1},{2,10},{10... | collective-permute-start | bytes 49160 | tf_op jit(solution)/shard_map/ppermute | solution.py:48
